TPU v7x, 32 devices: a whole 2x2x4 slice. The times are simulated.
32 devices in a mesh: vpair: 4 (over y, x), rank: 8 (over z, core).
Axes of the slice: x: 2, y: 2, z: 4, core: 2. Of those that a mesh axis runs over, the one named last changes fastest.
Arguments:
- amplitudes: bfloat16 [8, 1200, 1200], P(None, 'vpair', 'rank'), may hold values from -6 to 6
- factors: bfloat16 [1200, 8192], P('vpair', 'rank'), may hold values from -0.1875 to 0.1875
- kernel: bfloat16 [8192, 8192], P('vpair', 'rank'), may hold values from -0.875 to 0.875
- other_terms: float32 [8, 1200, 1200], P(None, 'vpair'), may hold values from -6 to 6
- virt_energy: float32 [1200], replicated, may hold values from 0.2 to 4
- pair_energy: float32 [8], replicated, may hold values from -3 to -0.5
Outputs:
- residual: float32 [8, 1200, 1200], P(None, 'vpair')
- update_rms: float32 [], replicated
All inputs are finite; a program needn't handle non-finite values.
Results may differ from a plain program's by a relative error of at most 0.0035.
Values may be sent and summed in bfloat16 or wider, within the bound.
A program may use at most 192 MiB of HBM per device.

v0:
```python
import functools

import jax
import jax.numpy as jnp
from jax import lax
from jax.experimental import pallas as pl
from jax.experimental.pallas import tpu as pltpu
from jax.sharding import PartitionSpec as P

epsilon = 1e-06


def shards(amplitudes, factors, kernel, other_terms, virt_energy, pair_energy):
    vpair_count = lax.axis_size("vpair")
    pair_count = amplitudes.shape[0]
    row_block = amplitudes.shape[1]
    col_block = amplitudes.shape[2]
    virt_count = row_block * vpair_count
    right_block = kernel.shape[1]
    factor_rows = lax.all_gather(factors, "rank", axis=1, tiled=True)
    factor_full = lax.all_gather(factor_rows, "vpair", axis=0, tiled=True)
    factor_cols = lax.dynamic_slice_in_dim(
        factor_full, lax.axis_index("rank") * right_block, right_block, 1
    )
    half_done = jnp.einsum(
        "ons,sh->onh",
        lax.all_gather(amplitudes, "rank", axis=2, tiled=True),
        factor_cols,
        preferred_element_type=jnp.float32,
    ).astype(jnp.bfloat16)
    kernel_sub = lax.all_to_all(kernel, "vpair", split_axis=1, concat_axis=0, tiled=True).astype(
        jnp.float32
    )
    coupled = jnp.einsum(
        "cp,icq->ipq",
        factor_full,
        lax.all_to_all(half_done, "vpair", split_axis=2, concat_axis=1, tiled=True),
        preferred_element_type=jnp.float32,
    )
    weighted = (kernel_sub[None] * coupled).astype(jnp.bfloat16)
    ladder_half = jnp.einsum(
        "ap,ipq->iaq", factor_full, weighted, preferred_element_type=jnp.float32
    ).astype(jnp.bfloat16)
    back_half = lax.all_to_all(ladder_half, "vpair", split_axis=1, concat_axis=2, tiled=True)
    partial_value = jnp.einsum(
        "iaq,bq->iab", back_half, factor_cols, preferred_element_type=jnp.float32
    )
    row_energy = lax.dynamic_slice_in_dim(
        virt_energy, lax.axis_index("vpair") * row_block, row_block, 0
    )
    ladder_share = lax.psum_scatter(partial_value, "rank", scatter_dimension=2, tiled=True)
    col_start = lax.axis_index("rank") * col_block
    own_terms = lax.dynamic_slice_in_dim(other_terms, col_start, col_block, 2)
    part_residual = own_terms + ladder_share
    col_energy = lax.dynamic_slice_in_dim(virt_energy, col_start, col_block, 0)
    denominator = row_energy[None, :, None] + col_energy[None, None, :] - pair_energy[:, None, None]
    update = part_residual / denominator
    squares = lax.psum(jnp.sum(update * update), ("vpair", "rank"))
    residual = lax.all_gather(part_residual, "rank", axis=2, tiled=True)
    update_rms = jnp.sqrt(squares / (pair_count * virt_count * virt_count) + epsilon)
    return (residual, update_rms)


def middle_kernel(
    zs, own_ref, half_ref, kern_ref, out_ref, gath_ref, fbuf, fturn, acc, mine_sem, load_sem, recv, s1, s2, s3
):
    v = lax.axis_index("vpair")
    r = lax.axis_index("rank")
    y, x = v // 2, v % 2
    z, core = r // 2, r % 2
    vx, vy, vd = y * 2 + 1 - x, (1 - y) * 2 + x, (1 - y) * 2 + 1 - x
    mate = z * 2 + 1 - core
    pairs, rows, cols = acc.shape
    depth = own_ref.shape[1]

    def rank_at(k):
        return ((z + k) % zs) * 2 + core

    barrier = pltpu.get_barrier_semaphore()
    peers = [(v, rank_at(k)) for k in range(1, zs)] + [(vx, r), (vy, r), (v, mate)]
    for peer in peers:
        pl.semaphore_signal(barrier, inc=1, device_id=peer, device_id_type=pl.DeviceIdType.MESH)
    pl.semaphore_wait(barrier, len(peers))

    started = []

    def send(src, rr, vv, sem, to):
        copy = pltpu.make_async_remote_copy(
            src_ref=src,
            dst_ref=gath_ref.at[rr, vv],
            send_sem=sem,
            recv_sem=recv.at[rr, vv],
            device_id=to,
            device_id_type=pl.DeviceIdType.MESH,
        )
        copy.start()
        started.append(copy)

    def arrived(rr, vv):
        pltpu.make_async_copy(gath_ref.at[rr, vv], gath_ref.at[rr, vv], recv.at[rr, vv]).wait()

    send(own_ref, r, v, s2.at[0, 0], (vx, r))
    send(own_ref, r, v, s2.at[0, 1], (vy, r))
    for k in range(1, zs):
        send(own_ref, r, v, s1.at[k], (v, rank_at(k)))
    send(own_ref, r, v, s3.at[0, 0], (v, mate))

    def spread(k):
        rr = rank_at(k)
        arrived(rr, v)
        shard = gath_ref.at[rr, v]
        send(shard, rr, v, s2.at[k, 0], (vx, r))
        send(shard, rr, v, s2.at[k, 1], (vy, r))
        send(shard, rr, v, s3.at[k, 0], (v, mate))

    def relay(k):
        rr = rank_at(k)
        odd = (rr // 2) % 2
        arrived(rr, vx)
        arrived(rr, vy)
        via = (y + odd * (1 - 2 * y)) * 2 + x + (1 - odd) * (1 - 2 * x)
        to = (y + (1 - odd) * (1 - 2 * y)) * 2 + x + odd * (1 - 2 * x)
        send(gath_ref.at[rr, via], rr, via, s2.at[k, 2], (to, r))
        send(gath_ref.at[rr, vx], rr, vx, s3.at[k, 1], (v, mate))
        send(gath_ref.at[rr, vy], rr, vy, s3.at[k, 2], (v, mate))

    def finish(k):
        rr = rank_at(k)
        arrived(rr, vd)
        send(gath_ref.at[rr, vd], rr, vd, s3.at[k, 3], (v, mate))

    def compute(slot, rr, first, tasks=()):
        start = pl.multiple_of(rr * depth, depth)

        @pl.loop(0, depth // 128)
        def _(c):
            piece = fbuf[slot, :, :, pl.ds(pl.multiple_of(c * 128, 128), 128)].reshape(rows, 128)
            fturn[pl.ds(pl.multiple_of(c * 128, 128), 128), :] = piece.T

        def one(i):
            half = half_ref[:, i].reshape(rows, cols)
            coupled = jnp.dot(fturn[...], half, preferred_element_type=jnp.float32)
            weight = kern_ref[pl.ds(start, depth), :].astype(jnp.float32)
            weighted = (weight * coupled).astype(jnp.bfloat16)
            term = jnp.dot(
                fbuf[slot].reshape(rows, depth), weighted, preferred_element_type=jnp.float32
            )
            if first:
                acc[i] = term
            else:
                acc[i] += term

        pieces = 4
        each = pairs // pieces
        for piece in range(pieces):
            if piece < len(tasks):
                tasks[piece]()
            pl.loop(piece * each, (piece + 1) * each)(one)

    def fetch(slot, rr):
        for j in range(4):
            pltpu.make_async_copy(gath_ref.at[rr, j], fbuf.at[slot, j], load_sem.at[slot, j]).start()

    def fetched(slot, rr):
        for j in range(4):
            pltpu.make_async_copy(gath_ref.at[rr, j], fbuf.at[slot, j], load_sem.at[slot, j]).wait()

    stage = fbuf.at[1, 0]
    into = pltpu.make_async_copy(own_ref, stage, mine_sem.at[0])
    into.start()
    into.wait()
    back = pltpu.make_async_copy(stage, gath_ref.at[r, v], mine_sem.at[1])
    back.start()
    back.wait()

    relay(0)
    spread(1)
    finish(0)
    fetch(0, r)
    queue = []
    for k in range(1, zs):
        if k + 1 < zs:
            queue.append(functools.partial(spread, k + 1))
        queue.append(functools.partial(relay, k))
        queue.append(functools.partial(finish, k))
    fetched(0, r)
    compute(0, r, True, queue[:4])
    queue = queue[4:]
    for k in range(zs):
        other = ((z + k) % zs) * 2 + 1 - core
        for at in (v, vx, vy, vd):
            arrived(other, at)
        fetch(1, other)
        if k + 1 < zs:
            fetch(0, rank_at(k + 1))
        fetched(1, other)
        compute(1, other, False, queue[:4])
        queue = queue[4:]
        if k + 1 < zs:
            fetched(0, rank_at(k + 1))
            compute(0, rank_at(k + 1), False, queue[:4])
            queue = queue[4:]
    for i in range(pairs):
        out_ref[:, i] = acc[i].reshape(4, rows // 4, cols).astype(jnp.bfloat16)
    for copy in started:
        copy.wait_send()


def front_kernel(zs, own_ref, amp_ref, cols_ref, amps_ref, mine_sem, cols_recv, amps_recv, cs, us, ds, ms, stage, hold):
    v = lax.axis_index("vpair")
    r = lax.axis_index("rank")
    y, x = v // 2, v % 2
    z, core = r // 2, r % 2
    near = (y * 2 + 1 - x, (1 - y) * 2 + x, (1 - y) * 2 + 1 - x)
    mate = z * 2 + 1 - core
    mesh_ids = pl.DeviceIdType.MESH
    has_up, has_down = z + 1 < zs, z >= 1
    up_to, down_to = ((z + 1) % zs) * 2 + core, ((z + zs - 1) % zs) * 2 + core

    barrier = pltpu.get_barrier_semaphore()
    peers = [(at, r) for at in near] + [(v, mate), (v, up_to), (v, down_to)]
    for peer in peers:
        pl.semaphore_signal(barrier, inc=1, device_id=peer, device_id_type=mesh_ids)
    pl.semaphore_wait(barrier, len(peers))

    def cols_copy(j, at, to):
        return pltpu.make_async_remote_copy(
            src_ref=own_ref, dst_ref=cols_ref.at[at], send_sem=cs.at[j], recv_sem=cols_recv.at[at],
            device_id=(to, r), device_id_type=mesh_ids,
        )

    def amps_copy(src, at, sem, to):
        return pltpu.make_async_remote_copy(
            src_ref=src, dst_ref=amps_ref.at[at], send_sem=sem, recv_sem=amps_recv.at[at],
            device_id=(v, to), device_id_type=mesh_ids,
        )

    def amps_wait(at):
        pltpu.make_async_copy(amps_ref.at[at], amps_ref.at[at], amps_recv.at[at]).wait()

    @pl.when(has_up)
    def _():
        amps_copy(amp_ref, r, us.at[0], up_to).start()

    @pl.when(has_down)
    def _():
        amps_copy(amp_ref, r, ds.at[0], down_to).start()

    for j in range(3):
        cols_copy(j, v, near[j]).start()
    amps_copy(amp_ref, r, ms.at[0, 0], mate).start()
    a = pltpu.make_async_copy(own_ref, stage, mine_sem.at[0])
    b = pltpu.make_async_copy(amp_ref, hold, mine_sem.at[1])
    a.start()
    b.start()
    a.wait()
    b.wait()
    c = pltpu.make_async_copy(stage, cols_ref.at[v], mine_sem.at[2])
    d = pltpu.make_async_copy(hold, amps_ref.at[r], mine_sem.at[3])
    c.start()
    d.start()
    c.wait()
    d.wait()

    for s in range(1, zs):
        low, high = ((z + zs - s) % zs) * 2 + core, ((z + s) % zs) * 2 + core

        @pl.when(z >= s)
        def _():
            amps_wait(low)
            amps_copy(amps_ref.at[low], low, ms.at[s, 0], mate).start()

            @pl.when(has_up)
            def _():
                amps_copy(amps_ref.at[low], low, us.at[s], up_to).start()

        @pl.when(z + s < zs)
        def _():
            amps_wait(high)
            amps_copy(amps_ref.at[high], high, ms.at[s, 1], mate).start()

            @pl.when(has_down)
            def _():
                amps_copy(amps_ref.at[high], high, ds.at[s], down_to).start()

    for at in near:
        pltpu.make_async_copy(cols_ref.at[at], cols_ref.at[at], cols_recv.at[at]).wait()
    for k in range(zs):
        amps_wait(k * 2 + 1 - core)
    for j in range(3):
        cols_copy(j, v, near[j]).wait_send()
    amps_copy(amp_ref, r, ms.at[0, 0], mate).wait_send()
    for s in range(zs):

        @pl.when(jnp.logical_and(z >= s, has_up))
        def _():
            amps_copy(amp_ref, r, us.at[s], up_to).wait_send()

        @pl.when(jnp.logical_and(z + s < zs, has_down))
        def _():
            amps_copy(amp_ref, r, ds.at[s], down_to).wait_send()

        if s:

            @pl.when(z >= s)
            def _():
                amps_copy(amp_ref, r, ms.at[s, 0], mate).wait_send()

            @pl.when(z + s < zs)
            def _():
                amps_copy(amp_ref, r, ms.at[s, 1], mate).wait_send()


def front_gather(factors_pad, amps_pad, vpair_count, rank_count):
    zs = rank_count // 2
    hbm = pl.BlockSpec(memory_space=pl.ANY)
    return pl.pallas_call(
        functools.partial(front_kernel, zs),
        out_shape=(
            jax.ShapeDtypeStruct((vpair_count, *factors_pad.shape), jnp.bfloat16),
            jax.ShapeDtypeStruct((rank_count, *amps_pad.shape), jnp.bfloat16),
        ),
        in_specs=[hbm, hbm],
        out_specs=(hbm, hbm),
        scratch_shapes=[
            pltpu.SemaphoreType.DMA((4,)),
            pltpu.SemaphoreType.DMA((vpair_count,)),
            pltpu.SemaphoreType.DMA((rank_count,)),
            pltpu.SemaphoreType.DMA((3,)),
            pltpu.SemaphoreType.DMA((zs,)),
            pltpu.SemaphoreType.DMA((zs,)),
            pltpu.SemaphoreType.DMA((zs, 2)),
            pltpu.VMEM(factors_pad.shape, jnp.bfloat16),
            pltpu.VMEM(amps_pad.shape, jnp.bfloat16),
        ],
        compiler_params=pltpu.CompilerParams(
            collective_id=1, has_side_effects=True, vmem_limit_bytes=60 * 1024 * 1024
        ),
        cost_estimate=pl.CostEstimate(flops=10**10, bytes_accessed=10**7, transcendentals=0),
    )(factors_pad, amps_pad)


def ladder_middle(factors_pad, half_sub, kernel_sub, rank_count):
    count, pairs, block, cols = half_sub.shape
    depth = factors_pad.shape[1]
    rows = count * block
    points = kernel_sub.shape[0]
    zs = rank_count // 2
    hbm = pl.BlockSpec(memory_space=pl.ANY)
    vmem = pl.BlockSpec(memory_space=pltpu.VMEM)
    return pl.pallas_call(
        functools.partial(middle_kernel, zs),
        out_shape=(
            jax.ShapeDtypeStruct((count, pairs, block, cols), jnp.bfloat16),
            jax.ShapeDtypeStruct((rank_count, count, block, depth), jnp.bfloat16),
        ),
        in_specs=[hbm, vmem, vmem],
        out_specs=(vmem, hbm),
        scratch_shapes=[
            pltpu.VMEM((2, count, block, depth), jnp.bfloat16),
            pltpu.VMEM((depth, rows), jnp.bfloat16),
            pltpu.VMEM((pairs, rows, cols), jnp.float32),
            pltpu.SemaphoreType.DMA((2,)),
            pltpu.SemaphoreType.DMA((2, count)),
            pltpu.SemaphoreType.DMA((rank_count, count)),
            pltpu.SemaphoreType.DMA((zs,)),
            pltpu.SemaphoreType.DMA((zs, 3)),
            pltpu.SemaphoreType.DMA((zs, 4)),
        ],
        compiler_params=pltpu.CompilerParams(
            collective_id=0, has_side_effects=True, vmem_limit_bytes=60 * 1024 * 1024
        ),
        cost_estimate=pl.CostEstimate(
            flops=4 * pairs * points * rows * cols, bytes_accessed=4 * points * rows, transcendentals=0
        ),
    )(factors_pad, half_sub, kernel_sub)


def fast_shards(amplitudes, factors, kernel, other_terms, virt_energy, pair_energy):
    vpair_count = lax.axis_size("vpair")
    rank_count = lax.axis_size("rank")
    pair_count, row_block, _ = amplitudes.shape
    virt_count = row_block * vpair_count
    right_block = kernel.shape[1]
    cols = right_block // vpair_count
    block = -(-row_block // 64) * 64
    col_block = amplitudes.shape[2]
    deep = -(-col_block // 16) * 16
    kernel_sub = lax.all_to_all(kernel, "vpair", split_axis=1, concat_axis=0, tiled=True)
    factors_pad = jnp.pad(factors, ((0, block - row_block), (0, 0)))
    amps_pad = jnp.pad(
        amplitudes.transpose(2, 0, 1), ((0, deep - col_block), (0, 0), (0, block - row_block))
    ).reshape(deep, pair_count * block)
    cols_pad, amps = front_gather(factors_pad, amps_pad, vpair_count, rank_count)
    factor_cols = cols_pad[:, :row_block].reshape(virt_count, right_block)
    cols_deep = jnp.pad(
        factor_cols.reshape(rank_count, col_block, right_block), ((0, 0), (0, deep - col_block), (0, 0))
    ).reshape(rank_count * deep, right_block)
    half_done = jnp.einsum(
        "sm,sh->mh",
        amps.reshape(rank_count * deep, pair_count * block),
        cols_deep,
        preferred_element_type=jnp.float32,
    ).astype(jnp.bfloat16)
    half_done = half_done.reshape(pair_count, block, vpair_count, cols).transpose(2, 0, 1, 3)
    half_sub = lax.all_to_all(half_done, "vpair", split_axis=0, concat_axis=0, tiled=True)
    back, _ = ladder_middle(factors_pad, half_sub, kernel_sub, rank_count)
    back = lax.all_to_all(back, "vpair", split_axis=0, concat_axis=0, tiled=True)
    back = back[:, :, :row_block]
    partial_value = jnp.einsum(
        "viaq,bvq->iab",
        back,
        factor_cols.reshape(virt_count, vpair_count, cols),
        preferred_element_type=jnp.float32,
    )
    ladder_own = lax.psum_scatter(partial_value, "rank", scatter_dimension=0, tiled=True)
    ladder = lax.all_gather(ladder_own.astype(jnp.bfloat16), "rank", axis=0, tiled=True)
    own = ladder_own.shape[0]
    start = lax.axis_index("rank") * own
    row_energy = lax.dynamic_slice_in_dim(
        virt_energy, lax.axis_index("vpair") * row_block, row_block, 0
    )
    own_terms = lax.optimization_barrier(lax.dynamic_slice_in_dim(other_terms, start, own, 0))
    own_pairs = lax.dynamic_slice_in_dim(pair_energy, start, own, 0)
    denominator = row_energy[None, :, None] + virt_energy[None, None, :] - own_pairs[:, None, None]
    update = (own_terms + ladder_own) / denominator
    squares = lax.psum(jnp.sum(update * update), ("vpair", "rank"))
    squares, ladder = lax.optimization_barrier((squares, ladder))
    turned = lax.optimization_barrier(ladder.transpose(1, 0, 2))
    residual = (other_terms.transpose(1, 0, 2) + turned.astype(jnp.float32)).transpose(1, 0, 2)
    update_rms = jnp.sqrt(squares / (pair_count * virt_count * virt_count) + epsilon)
    return (residual, update_rms)


def pick(amplitudes, factors, kernel, other_terms, virt_energy, pair_energy):
    vpair_count = lax.axis_size("vpair")
    rank_count = lax.axis_size("rank")
    fits = (
        vpair_count == 4
        and rank_count % 2 == 0
        and amplitudes.shape[0] % rank_count == 0
        and kernel.shape[1] % (128 * vpair_count) == 0
    )
    body = fast_shards if fits else shards
    return body(amplitudes, factors, kernel, other_terms, virt_energy, pair_energy)


def solution(mesh):
    placed = (
        P(None, "vpair", "rank"),
        P("vpair", "rank"),
        P("vpair", "rank"),
        P(None, "vpair", None),
        P(),
        P(),
    )
    return jax.shard_map(
        pick, mesh=mesh, in_specs=placed, out_specs=(P(None, "vpair", None), P()), check_vma=False
    )
```

profile of v0, /device:TPU:0, one launch (start us, length us, event | category | flops | bytes accessed | tf_op | source)
XLA Modules:
  0.0 815.8 jit_solution(7263429019054708823)
XLA Ops:
  7.2 4.5 copy.37
  11.7 5.3 all-to-all-start.1
  17.0 0.9 pad.12.own_ref
  18.0 1.5 reshape.70.amp_ref
  19.6 75.4 %shard_map.77 = (bf16[4,320,1024]{2,1,0:T(8,128)(2,1)}, bf16[8,160,2560]{2,1,0:T(8,128)(2,1)}) custom-call(bf16[320,1024]{1,0:T(8,128)(2,1)} %pad.12.own_ref, bf16[160,2560]{1,0:T(8,128)(2,1)} %reshape.70.amp_ref), custom_call_target="tpu_custom_call" | custom-call | flops 10000000000 | bytes 10000000 | tf_op jit(solution)/shard_map/pallas_call | solution.py:317
  95.0 1.9 slice.6
  97.0 2.2 reshape_reshape.6
  99.2 12.0 %bitcast_convert_fusion = bf16[2560,1024]{1,0:T(8,128)(2,1)} fusion(bf16[8,160,2560]{2,1,0:T(8,128)(2,1)} %get-tuple-element.7, bf16[8,150,1024]{2,1,0:T(8,128)(2,1)} %reshape_reshape.6), kind=kOutput, calls=%fused_computation.2 | convolution fusion | flops 6713507840 | bytes 14254080 | tf_op jit(solution)/shard_map/sm,sh->mh/dot_general | solution.py:399
  111.2 9.5 %reshape.71 = bf16[8,320,4,256]{3,2,1,0:T(4,128)(2,1)} reshape(bf16[2560,1024]{1,0:T(8,128)(2,1)} %bitcast_convert_fusion) | data formatting | bytes 10485760 | tf_op jit(solution)/shard_map/reshape | solution.py:405
  120.7 5.8 copy.36
  126.5 65.0 %all_to_all.29.half_ref = bf16[4,8,320,256]{3,2,1,0:T(8,128)(2,1)} all-to-all(bf16[4,8,320,256]{3,2,1,0:T(8,128)(2,1)} %bitcast.25), channel_id=1, replica_groups=mesh['vpair'=4,'rank'=8] {'vpair'}, dimensions={0} | all-to-all | bytes 10485760 | tf_op jit(solution)/shard_map/all_to_all | solution.py:406
  191.5 286.8 %shard_map.78 = (bf16[4,8,320,256]{3,2,1,0:T(8,128)(2,1)}, bf16[8,4,320,1024]{3,2,1,0:T(8,128)(2,1)}) custom-call(bf16[320,1024]{1,0:T(8,128)(2,1)} %pad.12.own_ref, bf16[4,8,320,256]{3,2,1,0:T(8,128)(2,1)} %all_to_all.29.half_ref, bf16[8192,256]{1,0:T(8,128)(2,1)} %bitcast.5.kern_ref), custom_call_target="tpu_custom_call" | custom-call | flops 85899345920 | bytes 41943040 | tf_op jit(solution)/shard_map/pallas_call | solution.py:351
  478.3 5.1 all-to-all-start.2
  483.4 2.6 reshape_reshape.7
  486.1 52.7 %all-to-all-done.2 = bf16[4,8,320,256]{3,2,1,0:T(8,128)(2,1)} async-done(((bf16[4,8,320,256]{3,2,1,0:T(8,128)(2,1)}), bf16[4,8,320,256]{3,2,1,0:T(8,128)(2,1)}, u32[]{:S(2)}, u32[]{:S(2)}) %all-to-all-start.2) | async-done | bytes 5242912 | tf_op jit(solution)/shard_map/all_to_all | solution.py:408
  538.8 12.0 %convolution_bitcast_fusion = f32[8,300,1200]{2,1,0:T(8,128)} fusion(bf16[4,8,320,256]{3,2,1,0:T(8,128)(2,1)} %all-to-all-done.2, bf16[1200,4,256,1]{2,1,0,3:T(4,128)(2,1)} %bitcast.29), kind=kOutput, calls=%fused_computation.3 | convolution fusion | flops 5898240000 | bytes 18958336 | tf_op jit(solution)/shard_map/viaq,bvq->iab/dot_general | solution.py:410
  550.8 12.9 %copy.21 = f32[8,300,1200]{2,1,0:T(8,128)} copy(f32[8,300,1200]{2,0,1:T(8,128)} %param.9) | data formatting | bytes 23040000 | tf_op args[3]
  564.3 1.5 constant_dynamic-slice_fusion
  565.9 141.4 %reduce-scatter.2.cloned.1.call-done = f32[1,300,1200]{2,1,0:T(8,128)} async-done(((f32[8,300,1200]{2,1,0:T(8,128)}), f32[1,300,1200]{2,1,0:T(8,128)}) %reduce-scatter.2.cloned.1.call-update) | async-done | bytes 1440016 | tf_op jit(solution)/shard_map/reduce_scatter | solution.py:416
  707.2 4.8 fusion.5
  712.0 42.7 %psum.7 = f32[]{:T(128)} all-reduce(f32[]{:T(128)} %get-tuple-element.19), channel_id=1, replica_groups=mesh['vpair'=4,'rank'=8] {'vpair','rank'}, use_global_device_ids=true, to_apply=%region_2.3 | all-reduce | flops 1 | bytes 8 | tf_op jit(solution)/shard_map/psum | solution.py:427
  754.7 21.1 %all-gather.2.cloned.1.call-done = bf16[8,300,1200]{2,1,0:T(8,128)(2,1)} async-done(((bf16[1,300,1200]{2,1,0:T(8,128)(2,1)}), bf16[8,300,1200]{2,1,0:T(8,128)(2,1)}) %all-gather.2.cloned.1.call-update) | async-done | bytes 5760016 | tf_op jit(solution)/shard_map/all_gather | solution.py:417
  775.8 14.8 %fusion = f32[8,300,1200]{2,1,0:T(8,128)} fusion(bf16[300,8,1200]{2,0,1:T(8,128)(2,1)} %bitcast.27, f32[8,300,1200]{2,0,1:T(8,128)} %param.9), kind=kLoop, calls=%fused_computation.1 | loop fusion | flops 5760000 | bytes 28800000 | tf_op jit(solution)/shard_map/transpose | solution.py:430
  790.6 16.3 %copy.26 = f32[8,300,1200]{2,0,1:T(8,128)} copy(f32[8,300,1200]{2,1,0:T(8,128)} %fusion) | data formatting | bytes 23040000
  (16 shorter events, 0.9 us)
Async XLA Ops:
  11.7 5.3 copy-start.1
  11.7 6.2 copy-start
  11.7 114.8 %all-to-all-start.1 = ((bf16[2048,4,256]{2,0,1:T(8,128)(2,1)}), bf16[2048,4,256]{2,0,1:T(8,128)(2,1)}, u32[]{:S(2)}, u32[]{:S(2)}) async-start(bf16[2048,4,256]{2,0,1:T(8,128)(2,1)} %bitcast.26), calls=%async_computation.1 | async-start | bytes 8388608 | tf_op jit(solution)/shard_map/all_to_all | solution.py:389
  478.3 60.5 %all-to-all-start.2 = ((bf16[4,8,320,256]{3,2,1,0:T(8,128)(2,1)}), bf16[4,8,320,256]{3,2,1,0:T(8,128)(2,1)}, u32[]{:S(2)}, u32[]{:S(2)}) async-start(bf16[4,8,320,256]{3,2,1,0:T(8,128)(2,1)} %get-tuple-element.9), calls=%async_computation.2 | async-start | bytes 10485760 | tf_op jit(solution)/shard_map/all_to_all | solution.py:408
  483.4 223.8 %reduce-scatter.2.cloned.1.call-start = ((), (), s32[]{:S(2)}) async-start(), calls=%async_computation.4 | async-start | bytes 14008320 | tf_op jit(solution)/shard_map/reduce_scatter | solution.py:416
  550.8 225.0 %all-gather.2.cloned.1.call-start = ((), (), s32[]{:S(2)}) async-start(), calls=%async_computation.5 | async-start | bytes 7004160 | tf_op jit(solution)/shard_map/all_gather | solution.py:417
  550.8 12.9 %copy-start.3 = (f32[8]{0:T(128)S(1)}, f32[8]{0:T(128)}, u32[]{:S(2)}) copy-start(f32[8]{0:T(128)} %param.11) | copy-start | bytes 100
  550.8 15.0 %copy-start.2 = (f32[1200]{0:T(1024)S(1)}, f32[1200]{0:T(1024)}, u32[]{:S(2)}) copy-start(f32[1200]{0:T(1024)} %param.10) | copy-start | bytes 14404
Sparse Core Ops, SparseCore 0:
  550.9 156.3 reduce-scatter.1
  712.2 63.6 all-gather.1
where the time goes:
time: 822 us; the launch traced here: 816 us
  Pallas kernels  362 us (44%)
  waiting for transfers between devices  215 us (26%)
  blocking collectives  108 us (13%)
  local copies, waits for them, and re-layouts  60.5 us (7%)
  matrix products  24 us (3%)
  other arithmetic  19.5 us (2%)
  between operations  16.1 us (2%)
  starting transfers between devices  10.5 us (1%)
    pallas_call x1, Pallas kernels, ladder_middle(): pl.pallas_call(functools.partial(middle_kernel, zs), out_shape=(jax.Shape...  287 us
    reduce_scatter x1, waiting for transfers between devices, fast_shards(): lax.psum_scatter(partial_value, 'rank', scatter_dimension=0, tiled=True)  141 us
    pallas_call x1, Pallas kernels, front_gather(): pl.pallas_call(functools.partial(front_kernel, zs), out_shape=(jax.ShapeD...  75.4 us
    all_to_all x1, blocking collectives, fast_shards(): lax.all_to_all(half_done, 'vpair', split_axis=0, concat_axis=0, tiled=True)  65 us
    all_to_all x1, waiting for transfers between devices, fast_shards(): lax.all_to_all(back, 'vpair', split_axis=0, concat_axis=0, tiled=True)  52.7 us
    psum x1, blocking collectives, fast_shards(): squares = lax.psum(jnp.sum(update * update), ('vpair', 'rank'))  42.7 us
    unnamed x10, local copies, waits for them, and re-layouts  29.2 us
    all_gather x1, waiting for transfers between devices, fast_shards(): lax.all_gather(ladder_own.astype(jnp.bfloat16), 'rank', axis=0, tiled=True)  21.1 us
  transfers between devices with their start and end apart: 4, of which 3 were waited for; matrix products, arithmetic and copies ran while one was open for 6% of the time, Pallas kernels for 9%

commit v1 on v0

--- a/solution.py
+++ b/solution.py
@@ -61,149 +61,194 @@
     return (residual, update_rms)
 
 
+MESH_IDS = pl.DeviceIdType.MESH
+
+
 def middle_kernel(
-    zs, own_ref, half_ref, kern_ref, out_ref, gath_ref, fbuf, fturn, acc, mine_sem, load_sem, recv, s1, s2, s3
+    zs, own_ref, cols_ref, half_ref, kern_ref, out_ref, fall, hrecv, hturn, kturn, acc,
+    loc_sem, hs, hr, fr, mr, zsend, xsend, msend, osem,
 ):
     v = lax.axis_index("vpair")
     r = lax.axis_index("rank")
     y, x = v // 2, v % 2
     z, core = r // 2, r % 2
     vx, vy, vd = y * 2 + 1 - x, (1 - y) * 2 + x, (1 - y) * 2 + 1 - x
+    near = (vx, vy, vd)
     mate = z * 2 + 1 - core
-    pairs, rows, cols = acc.shape
+    pairs, count, block, cols = hrecv.shape
     depth = own_ref.shape[1]
-
-    def rank_at(k):
-        return ((z + k) % zs) * 2 + core
+    rows = count * block
+    group = 2
+    groups = pairs // group
+    tall = group * cols
+
+    def rank_at(k, side):
+        return ((z + k) % zs) * 2 + side
 
     barrier = pltpu.get_barrier_semaphore()
-    peers = [(v, rank_at(k)) for k in range(1, zs)] + [(vx, r), (vy, r), (v, mate)]
+    peers = [(v, rank_at(k, core)) for k in range(1, zs)] + [(at, r) for at in near] + [(v, mate)]
     for peer in peers:
-        pl.semaphore_signal(barrier, inc=1, device_id=peer, device_id_type=pl.DeviceIdType.MESH)
+        pl.semaphore_signal(barrier, inc=1, device_id=peer, device_id_type=MESH_IDS)
     pl.semaphore_wait(barrier, len(peers))
 
-    started = []
-
-    def send(src, rr, vv, sem, to):
-        copy = pltpu.make_async_remote_copy(
-            src_ref=src,
-            dst_ref=gath_ref.at[rr, vv],
-            send_sem=sem,
-            recv_sem=recv.at[rr, vv],
-            device_id=to,
-            device_id_type=pl.DeviceIdType.MESH,
+    def remote(src, dst, send_sem, recv_sem, to):
+        return pltpu.make_async_remote_copy(
+            src_ref=src, dst_ref=dst, send_sem=send_sem, recv_sem=recv_sem,
+            device_id=to, device_id_type=MESH_IDS,
         )
-        copy.start()
-        started.append(copy)
-
-    def arrived(rr, vv):
-        pltpu.make_async_copy(gath_ref.at[rr, vv], gath_ref.at[rr, vv], recv.at[rr, vv]).wait()
-
-    send(own_ref, r, v, s2.at[0, 0], (vx, r))
-    send(own_ref, r, v, s2.at[0, 1], (vy, r))
-    for k in range(1, zs):
-        send(own_ref, r, v, s1.at[k], (v, rank_at(k)))
-    send(own_ref, r, v, s3.at[0, 0], (v, mate))
+
+    def half_copy(i, j):
+        at = pl.multiple_of(near[j] * cols, cols)
+        return remote(
+            half_ref.at[i, :, pl.ds(at, cols)], hrecv.at[i, v], hs.at[i, j], hr.at[i, v], (near[j], r)
+        )
+
+    def own_half(i):
+        at = pl.multiple_of(v * cols, cols)
+        return pltpu.make_async_copy(half_ref.at[i, :, pl.ds(at, cols)], hrecv.at[i, v], hr.at[i, v])
+
+    def rows_copy(k):
+        return remote(own_ref, fall.at[r, v], zsend.at[k], fr.at[r, v], (v, rank_at(k, core)))
+
+    def side_copy(rr, at, k, j, to):
+        return remote(fall.at[rr, at], fall.at[rr, at], xsend.at[k, j], fr.at[rr, at], (to, r))
+
+    def mate_copy(k):
+        rr = rank_at(k, core)
+        return remote(fall.at[rr], fall.at[rr], msend.at[k], mr.at[rr], (v, mate))
+
+    def shard_wait(rr, at):
+        pltpu.make_async_copy(fall.at[rr, at], fall.at[rr, at], fr.at[rr, at]).wait()
+
+    def block_wait(rr):
+        pltpu.make_async_copy(fall.at[rr], fall.at[rr], mr.at[rr]).wait()
 
     def spread(k):
-        rr = rank_at(k)
-        arrived(rr, v)
-        shard = gath_ref.at[rr, v]
-        send(shard, rr, v, s2.at[k, 0], (vx, r))
-        send(shard, rr, v, s2.at[k, 1], (vy, r))
-        send(shard, rr, v, s3.at[k, 0], (v, mate))
-
-    def relay(k):
-        rr = rank_at(k)
+        rr = rank_at(k, core)
+        shard_wait(rr, v)
+        side_copy(rr, v, k, 0, vx).start()
+        side_copy(rr, v, k, 1, vy).start()
+
+    def relay_copy(k):
+        rr = rank_at(k, core)
         odd = (rr // 2) % 2
-        arrived(rr, vx)
-        arrived(rr, vy)
         via = (y + odd * (1 - 2 * y)) * 2 + x + (1 - odd) * (1 - 2 * x)
         to = (y + (1 - odd) * (1 - 2 * y)) * 2 + x + odd * (1 - 2 * x)
-        send(gath_ref.at[rr, via], rr, via, s2.at[k, 2], (to, r))
-        send(gath_ref.at[rr, vx], rr, vx, s3.at[k, 1], (v, mate))
-        send(gath_ref.at[rr, vy], rr, vy, s3.at[k, 2], (v, mate))
+        return side_copy(rr, via, k, 2, to)
+
+    def relay(k):
+        rr = rank_at(k, core)
+        shard_wait(rr, vx)
+        shard_wait(rr, vy)
+        relay_copy(k).start()
 
     def finish(k):
-        rr = rank_at(k)
-        arrived(rr, vd)
-        send(gath_ref.at[rr, vd], rr, vd, s3.at[k, 3], (v, mate))
-
-    def compute(slot, rr, first, tasks=()):
+        shard_wait(rank_at(k, core), vd)
+        mate_copy(k).start()
+
+    own_block = pltpu.make_async_copy(cols_ref, fall.at[r], loc_sem.at[0])
+    mate_block = remote(cols_ref, fall.at[r], msend.at[0], mr.at[r], (v, mate))
+    own_block.start()
+    mate_block.start()
+    for k in range(1, zs):
+        rows_copy(k).start()
+
+    @pl.loop(0, pairs)
+    def _(i):
+        for j in (0, 1, 2):
+            half_copy(i, j).start()
+        own_half(i).start()
+
+    def turn_kernel(rr, slot):
         start = pl.multiple_of(rr * depth, depth)
-
-        @pl.loop(0, depth // 128)
-        def _(c):
-            piece = fbuf[slot, :, :, pl.ds(pl.multiple_of(c * 128, 128), 128)].reshape(rows, 128)
-            fturn[pl.ds(pl.multiple_of(c * 128, 128), 128), :] = piece.T
-
-        def one(i):
-            half = half_ref[:, i].reshape(rows, cols)
-            coupled = jnp.dot(fturn[...], half, preferred_element_type=jnp.float32)
-            weight = kern_ref[pl.ds(start, depth), :].astype(jnp.float32)
-            weighted = (weight * coupled).astype(jnp.bfloat16)
-            term = jnp.dot(
-                fbuf[slot].reshape(rows, depth), weighted, preferred_element_type=jnp.float32
-            )
-            if first:
-                acc[i] = term
-            else:
-                acc[i] += term
-
-        pieces = 4
-        each = pairs // pieces
-        for piece in range(pieces):
-            if piece < len(tasks):
-                tasks[piece]()
-            pl.loop(piece * each, (piece + 1) * each)(one)
-
-    def fetch(slot, rr):
-        for j in range(4):
-            pltpu.make_async_copy(gath_ref.at[rr, j], fbuf.at[slot, j], load_sem.at[slot, j]).start()
-
-    def fetched(slot, rr):
-        for j in range(4):
-            pltpu.make_async_copy(gath_ref.at[rr, j], fbuf.at[slot, j], load_sem.at[slot, j]).wait()
-
-    stage = fbuf.at[1, 0]
-    into = pltpu.make_async_copy(own_ref, stage, mine_sem.at[0])
-    into.start()
-    into.wait()
-    back = pltpu.make_async_copy(stage, gath_ref.at[r, v], mine_sem.at[1])
-    back.start()
-    back.wait()
-
-    relay(0)
-    spread(1)
-    finish(0)
-    fetch(0, r)
-    queue = []
+        kturn[slot] = kern_ref[pl.ds(start, depth), :].T
+
+    def compute(rr, slot, g):
+        at = pl.multiple_of(g * tall, tall)
+        shard = fall[rr].reshape(rows, depth)
+        coupled = jnp.dot(hturn[pl.ds(at, tall), :], shard, preferred_element_type=jnp.float32)
+        weight = kturn[slot].astype(jnp.float32)
+        weighted = (coupled.reshape(group, cols, depth) * weight[None]).astype(jnp.bfloat16)
+        return lax.dot_general(
+            weighted.reshape(tall, depth), shard, (((1,), (1,)), ((), ())),
+            preferred_element_type=jnp.float32,
+        )
+
+    turn_kernel(r, 0)
+    turn_kernel(mate, 1)
+    own_block.wait()
+    block_wait(mate)
+
+    @pl.loop(0, groups)
+    def _(g):
+        at = pl.multiple_of(g * tall, tall)
+        for e in range(group):
+            i = g * group + e
+            for j in range(count):
+                pltpu.make_async_copy(hrecv.at[i, j], hrecv.at[i, j], hr.at[i, j]).wait()
+            hturn[pl.ds(at + e * cols, cols), :] = hrecv[i].reshape(rows, cols).T
+        acc[pl.ds(at, tall), :] = compute(r, 0, g)
+        acc[pl.ds(at, tall), :] += compute(mate, 1, g)
+
+        @pl.when(g == 1)
+        def _():
+            spread(1)
+
+    relay(1)
+    spread(2)
+    finish(1)
+
+    @pl.loop(0, 2 * (zs - 1))
+    def _(n):
+        k = n // 2 + 1
+        odd = n % 2
+        rr = rank_at(k, core + odd - 2 * odd * core)
+
+        @pl.when(odd == 1)
+        def _():
+            block_wait(rr)
+
+        turn_kernel(rr, 0)
+
+        @pl.loop(0, groups)
+        def _(g):
+            @pl.when(jnp.logical_and(k < zs - 1, jnp.logical_and(odd == 0, g == 1)))
+            def _():
+                relay(k + 1)
+
+                @pl.when(k < zs - 2)
+                def _():
+                    spread(k + 2)
+
+            @pl.when(jnp.logical_and(k < zs - 1, jnp.logical_and(odd == 1, g == 0)))
+            def _():
+                finish(k + 1)
+
+            at = pl.multiple_of(g * tall, tall)
+            acc[pl.ds(at, tall), :] += compute(rr, 0, g)
+
+    def give(i):
+        return pltpu.make_async_copy(hrecv.at[i], out_ref.at[i], osem.at[i])
+
+    @pl.loop(0, pairs)
+    def _(i):
+        at = pl.multiple_of(i * cols, cols)
+        hrecv[i] = acc[pl.ds(at, cols), :].astype(jnp.bfloat16).T.reshape(count, block, cols)
+        give(i).start()
+
+    mate_block.wait_send()
     for k in range(1, zs):
-        if k + 1 < zs:
-            queue.append(functools.partial(spread, k + 1))
-        queue.append(functools.partial(relay, k))
-        queue.append(functools.partial(finish, k))
-    fetched(0, r)
-    compute(0, r, True, queue[:4])
-    queue = queue[4:]
-    for k in range(zs):
-        other = ((z + k) % zs) * 2 + 1 - core
-        for at in (v, vx, vy, vd):
-            arrived(other, at)
-        fetch(1, other)
-        if k + 1 < zs:
-            fetch(0, rank_at(k + 1))
-        fetched(1, other)
-        compute(1, other, False, queue[:4])
-        queue = queue[4:]
-        if k + 1 < zs:
-            fetched(0, rank_at(k + 1))
-            compute(0, rank_at(k + 1), False, queue[:4])
-            queue = queue[4:]
-    for i in range(pairs):
-        out_ref[:, i] = acc[i].reshape(4, rows // 4, cols).astype(jnp.bfloat16)
-    for copy in started:
-        copy.wait_send()
+        rows_copy(k).wait_send()
+        side_copy(r, v, k, 0, vx).wait_send()
+        side_copy(r, v, k, 1, vy).wait_send()
+        relay_copy(k).wait_send()
+        mate_copy(k).wait_send()
+
+    @pl.loop(0, pairs)
+    def _(i):
+        for j in (0, 1, 2):
+            half_copy(i, j).wait_send()
+        give(i).wait()
 
 
 def front_kernel(zs, own_ref, amp_ref, cols_ref, amps_ref, mine_sem, cols_recv, amps_recv, cs, us, ds, ms, stage, hold):
@@ -340,40 +385,317 @@
     )(factors_pad, amps_pad)
 
 
-def ladder_middle(factors_pad, half_sub, kernel_sub, rank_count):
-    count, pairs, block, cols = half_sub.shape
-    depth = factors_pad.shape[1]
+def ladder_middle(factors_pad, cols_pad, half_done, kernel_sub, rank_count):
+    count, block, depth = cols_pad.shape
+    pairs = half_done.shape[0]
+    cols = kernel_sub.shape[1]
     rows = count * block
     points = kernel_sub.shape[0]
     zs = rank_count // 2
     hbm = pl.BlockSpec(memory_space=pl.ANY)
     vmem = pl.BlockSpec(memory_space=pltpu.VMEM)
+    dma = pltpu.SemaphoreType.DMA
     return pl.pallas_call(
         functools.partial(middle_kernel, zs),
-        out_shape=(
-            jax.ShapeDtypeStruct((count, pairs, block, cols), jnp.bfloat16),
-            jax.ShapeDtypeStruct((rank_count, count, block, depth), jnp.bfloat16),
-        ),
-        in_specs=[hbm, vmem, vmem],
-        out_specs=(vmem, hbm),
+        out_shape=jax.ShapeDtypeStruct((pairs, count, block, cols), jnp.bfloat16),
+        in_specs=[hbm, hbm, hbm, vmem],
+        out_specs=hbm,
         scratch_shapes=[
-            pltpu.VMEM((2, count, block, depth), jnp.bfloat16),
-            pltpu.VMEM((depth, rows), jnp.bfloat16),
-            pltpu.VMEM((pairs, rows, cols), jnp.float32),
-            pltpu.SemaphoreType.DMA((2,)),
-            pltpu.SemaphoreType.DMA((2, count)),
-            pltpu.SemaphoreType.DMA((rank_count, count)),
-            pltpu.SemaphoreType.DMA((zs,)),
-            pltpu.SemaphoreType.DMA((zs, 3)),
-            pltpu.SemaphoreType.DMA((zs, 4)),
+            pltpu.VMEM((rank_count, count, block, depth), jnp.bfloat16),
+            pltpu.VMEM((pairs, count, block, cols), jnp.bfloat16),
+            pltpu.VMEM((pairs * cols, rows), jnp.bfloat16),
+            pltpu.VMEM((2, cols, depth), jnp.bfloat16),
+            pltpu.VMEM((pairs * cols, rows), jnp.float32),
+            dma((1,)),
+            dma((pairs, 3)),
+            dma((pairs, count)),
+            dma((rank_count, count)),
+            dma((rank_count,)),
+            dma((zs,)),
+            dma((zs, 3)),
+            dma((zs,)),
+            dma((pairs,)),
         ],
         compiler_params=pltpu.CompilerParams(
-            collective_id=0, has_side_effects=True, vmem_limit_bytes=60 * 1024 * 1024
+            collective_id=0, has_side_effects=True, vmem_limit_bytes=62 * 1024 * 1024
         ),
         cost_estimate=pl.CostEstimate(
             flops=4 * pairs * points * rows * cols, bytes_accessed=4 * points * rows, transcendentals=0
         ),
-    )(factors_pad, half_sub, kernel_sub)
+    )(factors_pad, cols_pad, half_done, kernel_sub)
+
+
+def tail_kernel(
+    back_ref, cols_ref, other_ref, rowen_ref, virt_ref, res_ref, sq_ref,
+    rb, turned, part, msend, mrecv, zsend, outer, inner, fin, oth, sq, sqall,
+    bs, br, ms, mr, zs_sem, outr, inr, fs, fr, osem, rsem, qs, qr,
+):
+    v = lax.axis_index("vpair")
+    r = lax.axis_index("rank")
+    y, x = v // 2, v % 2
+    z, core = r // 2, r % 2
+    near = (y * 2 + 1 - x, (1 - y) * 2 + x, (1 - y) * 2 + 1 - x)
+    mate = z * 2 + 1 - core
+    pairs, count, block, cols = rb.shape
+    rows = part.shape[1]
+    turns = pairs // 2
+    at_end = jnp.logical_or(z == 0, z == 3)
+    in_middle = jnp.logical_not(at_end)
+    toward = jnp.where(z < 2, z + 1, z - 1)
+    away = jnp.where(z == 1, 0, 3)
+    toward_at = (v, toward * 2 + core)
+    away_at = (v, away * 2 + core)
+    mate_at = (v, mate)
+
+    barrier = pltpu.get_barrier_semaphore()
+    for peer in [(at, r) for at in near] + [mate_at, toward_at]:
+        pl.semaphore_signal(barrier, inc=1, device_id=peer, device_id_type=MESH_IDS)
+
+    @pl.when(in_middle)
+    def _():
+        pl.semaphore_signal(barrier, inc=1, device_id=away_at, device_id_type=MESH_IDS)
+        pl.semaphore_wait(barrier, 6)
+
+    @pl.when(at_end)
+    def _():
+        pl.semaphore_wait(barrier, 5)
+
+    def remote(src, dst, send_sem, recv_sem, to):
+        return pltpu.make_async_remote_copy(
+            src_ref=src, dst_ref=dst, send_sem=send_sem, recv_sem=recv_sem,
+            device_id=to, device_id_type=MESH_IDS,
+        )
+
+    def arrive(ref, sem):
+        pltpu.make_async_copy(ref, ref, sem).wait()
+
+    def back_copy(i, j):
+        return remote(back_ref.at[i, near[j]], rb.at[i, v], bs.at[i, j], br.at[i, v], (near[j], r))
+
+    def own_back(i):
+        return pltpu.make_async_copy(back_ref.at[i, v], rb.at[i, v], br.at[i, v])
+
+    @pl.loop(0, pairs)
+    def _(i):
+        for j in range(3):
+            back_copy(i, j).start()
+        own_back(i).start()
+
+    def other_copy(p):
+        return pltpu.make_async_copy(other_ref.at[:, p], oth.at[p % 4], osem.at[p % 4])
+
+    def res_copy(p):
+        return pltpu.make_async_copy(oth.at[p % 4], res_ref.at[:, p], rsem.at[p % 4])
+
+    other_copy(0).start()
+    other_copy(1).start()
+    turned[...] = cols_ref[...].T
+
+    def mate_copy(t):
+        return remote(msend.at[t], mrecv.at[t], ms.at[t], mr.at[t], mate_at)
+
+    def outer_copy(t):
+        return remote(zsend.at[t], outer.at[t], zs_sem.at[t], outr.at[t], toward_at)
+
+    def inner_copy(t):
+        return remote(zsend.at[t], inner.at[t], zs_sem.at[t], inr.at[t], toward_at)
+
+    def fin_copy(p, j, to):
+        return remote(fin.at[p], fin.at[p], fs.at[p // 2, j], fr.at[p], to)
+
+    def ladder(p):
+        for j in range(count):
+            arrive(rb.at[p, j], br.at[p, j])
+        left = jnp.concatenate([rb[p, j] for j in range(count)], axis=1)
+        return jnp.dot(left, turned[...], preferred_element_type=jnp.float32)[:rows]
+
+    def step_a(t):
+        msend[t] = ladder(2 * t + 1 - core).astype(jnp.bfloat16)
+        mate_copy(t).start()
+        part[t] = ladder(2 * t + core)
+
+    def step_b(t):
+        arrive(mrecv.at[t], mr.at[t])
+        both = part[t] + mrecv[t].astype(jnp.float32)
+
+        @pl.when(at_end)
+        def _():
+            zsend[t] = both.astype(jnp.bfloat16)
+            outer_copy(t).start()
+
+        @pl.when(in_middle)
+        def _():
+            part[t] = both
+
+    def owner(t):
+        return z == 1 + t % 2
+
+    def step_c(t):
+        @pl.when(in_middle)
+        def _():
+            arrive(outer.at[t], outr.at[t])
+            three = part[t] + outer[t].astype(jnp.float32)
+
+            @pl.when(owner(t))
+            def _():
+                part[t] = three
+
+            @pl.when(jnp.logical_not(owner(t)))
+            def _():
+                zsend[t] = three.astype(jnp.bfloat16)
+                inner_copy(t).start()
+
+    def step_d(t):
+        p = 2 * t + core
+
+        @pl.when(jnp.logical_and(in_middle, owner(t)))
+        def _():
+            arrive(inner.at[t], inr.at[t])
+            fin[p] = (part[t] + inner[t].astype(jnp.float32)).astype(jnp.bfloat16)
+            fin_copy(p, 0, away_at).start()
+            fin_copy(p, 1, toward_at).start()
+            fin_copy(p, 2, mate_at).start()
+
+        @pl.when(jnp.logical_and(in_middle, jnp.logical_not(owner(t))))
+        def _():
+            arrive(fin.at[p], fr.at[p])
+            fin_copy(p, 0, away_at).start()
+            fin_copy(p, 2, mate_at).start()
+
+    def step_e(t):
+        p = 2 * t + core
+
+        @pl.when(at_end)
+        def _():
+            arrive(fin.at[p], fr.at[p])
+            fin_copy(p, 2, mate_at).start()
+
+    def settle(p):
+        other_copy(p).wait()
+        value = oth[p % 4] + fin[p].astype(jnp.float32)
+        oth[p % 4] = value
+        update = value / (rowen_ref[p] + virt_ref[...])
+        sq[pl.ds(p, 1), :] = jnp.sum(update * update, axis=0, keepdims=True)
+        res_copy(p).start()
+
+    def step_f(t):
+        arrive(fin.at[2 * t + 1 - core], fr.at[2 * t + 1 - core])
+
+        @pl.when(t + 1 < turns)
+        def _():
+            for e in range(2):
+                p = 2 * t + 2 + e
+
+                @pl.when(t > 0)
+                def _():
+                    res_copy(p).wait()
+
+                other_copy(p).start()
+
+        for e in range(2):
+            settle(2 * t + e)
+
+    @pl.loop(0, turns + 5)
+    def _(u):
+        for lag, step in enumerate((step_a, step_b, step_c, step_d, step_e, step_f)):
+
+            @pl.when(jnp.logical_and(u >= lag, u < turns + lag))
+            def _():
+                step(u - lag)
+
+    sqall[v] = sq[...]
+    for j in range(3):
+        remote(sq, sqall.at[v], qs.at[j], qr.at[v], (near[j], r)).start()
+    for at in near:
+        arrive(sqall.at[at], qr.at[at])
+    total = (sqall[0] + sqall[1]) + (sqall[2] + sqall[3])
+    sq_ref[...] = jnp.sum(jnp.sum(total, axis=1, keepdims=True), axis=0, keepdims=True)
+
+    for j in range(3):
+        remote(sq, sqall.at[v], qs.at[j], qr.at[v], (near[j], r)).wait_send()
+
+    @pl.loop(0, pairs)
+    def _(i):
+        for j in range(3):
+            back_copy(i, j).wait_send()
+
+    @pl.loop(0, turns)
+    def _(t):
+        p = 2 * t + core
+        mate_copy(t).wait_send()
+        fin_done = jnp.logical_and(in_middle, owner(t))
+
+        @pl.when(jnp.logical_not(fin_done))
+        def _():
+            outer_copy(t).wait_send()
+
+        @pl.when(in_middle)
+        def _():
+            fin_copy(p, 0, away_at).wait_send()
+
+        @pl.when(fin_done)
+        def _():
+            fin_copy(p, 1, toward_at).wait_send()
+
+        fin_copy(p, 2, mate_at).wait_send()
+
+    for p in range(pairs - 4, pairs):
+        res_copy(p).wait()
+
+
+def ladder_tail(back, cols_flat, other_turned, row_energy, virt_energy):
+    pairs, count, block, cols = back.shape
+    rows = other_turned.shape[0]
+    virt_count, depth = cols_flat.shape
+    turns = pairs // 2
+    hbm = pl.BlockSpec(memory_space=pl.ANY)
+    vmem = pl.BlockSpec(memory_space=pltpu.VMEM)
+    dma = pltpu.SemaphoreType.DMA
+    bf16 = lambda *shape: pltpu.VMEM(shape, jnp.bfloat16)
+    f32 = lambda *shape: pltpu.VMEM(shape, jnp.float32)
+    return pl.pallas_call(
+        tail_kernel,
+        out_shape=(
+            jax.ShapeDtypeStruct((rows, pairs, virt_count), jnp.float32),
+            jax.ShapeDtypeStruct((1, 1), jnp.float32),
+        ),
+        in_specs=[hbm, vmem, hbm, vmem, vmem],
+        out_specs=(hbm, vmem),
+        scratch_shapes=[
+            bf16(pairs, count, block, cols),
+            bf16(depth, virt_count),
+            f32(turns, rows, virt_count),
+            bf16(turns, rows, virt_count),
+            bf16(turns, rows, virt_count),
+            bf16(turns, rows, virt_count),
+            bf16(turns, rows, virt_count),
+            bf16(turns, rows, virt_count),
+            bf16(pairs, rows, virt_count),
+            f32(4, rows, virt_count),
+            f32(pairs, virt_count),
+            f32(count, pairs, virt_count),
+            dma((pairs, 3)),
+            dma((pairs, count)),
+            dma((turns,)),
+            dma((turns,)),
+            dma((turns,)),
+            dma((turns,)),
+            dma((turns,)),
+            dma((turns, 3)),
+            dma((pairs,)),
+            dma((4,)),
+            dma((4,)),
+            dma((3,)),
+            dma((count,)),
+        ],
+        compiler_params=pltpu.CompilerParams(
+            collective_id=2, has_side_effects=True, vmem_limit_bytes=62 * 1024 * 1024
+        ),
+        cost_estimate=pl.CostEstimate(
+            flops=2 * pairs * rows * virt_count * depth, bytes_accessed=8 * pairs * rows * virt_count,
+            transcendentals=0,
+        ),
+    )(back, cols_flat, other_turned, row_energy, virt_energy)
 
 
 def fast_shards(amplitudes, factors, kernel, other_terms, virt_energy, pair_energy):
@@ -382,8 +704,7 @@
     pair_count, row_block, _ = amplitudes.shape
     virt_count = row_block * vpair_count
     right_block = kernel.shape[1]
-    cols = right_block // vpair_count
-    block = -(-row_block // 64) * 64
+    block = -(-row_block // 16) * 16
     col_block = amplitudes.shape[2]
     deep = -(-col_block // 16) * 16
     kernel_sub = lax.all_to_all(kernel, "vpair", split_axis=1, concat_axis=0, tiled=True)
@@ -402,34 +723,17 @@
         cols_deep,
         preferred_element_type=jnp.float32,
     ).astype(jnp.bfloat16)
-    half_done = half_done.reshape(pair_count, block, vpair_count, cols).transpose(2, 0, 1, 3)
-    half_sub = lax.all_to_all(half_done, "vpair", split_axis=0, concat_axis=0, tiled=True)
-    back, _ = ladder_middle(factors_pad, half_sub, kernel_sub, rank_count)
-    back = lax.all_to_all(back, "vpair", split_axis=0, concat_axis=0, tiled=True)
-    back = back[:, :, :row_block]
-    partial_value = jnp.einsum(
-        "viaq,bvq->iab",
-        back,
-        factor_cols.reshape(virt_count, vpair_count, cols),
-        preferred_element_type=jnp.float32,
-    )
-    ladder_own = lax.psum_scatter(partial_value, "rank", scatter_dimension=0, tiled=True)
-    ladder = lax.all_gather(ladder_own.astype(jnp.bfloat16), "rank", axis=0, tiled=True)
-    own = ladder_own.shape[0]
-    start = lax.axis_index("rank") * own
+    half_done = half_done.reshape(pair_count, block, right_block)
+    back = ladder_middle(factors_pad, cols_pad, half_done, kernel_sub, rank_count)
     row_energy = lax.dynamic_slice_in_dim(
         virt_energy, lax.axis_index("vpair") * row_block, row_block, 0
     )
-    own_terms = lax.optimization_barrier(lax.dynamic_slice_in_dim(other_terms, start, own, 0))
-    own_pairs = lax.dynamic_slice_in_dim(pair_energy, start, own, 0)
-    denominator = row_energy[None, :, None] + virt_energy[None, None, :] - own_pairs[:, None, None]
-    update = (own_terms + ladder_own) / denominator
-    squares = lax.psum(jnp.sum(update * update), ("vpair", "rank"))
-    squares, ladder = lax.optimization_barrier((squares, ladder))
-    turned = lax.optimization_barrier(ladder.transpose(1, 0, 2))
-    residual = (other_terms.transpose(1, 0, 2) + turned.astype(jnp.float32)).transpose(1, 0, 2)
-    update_rms = jnp.sqrt(squares / (pair_count * virt_count * virt_count) + epsilon)
-    return (residual, update_rms)
+    shifted = row_energy[None, :, None] - pair_energy[:, None, None]
+    residual, squares = ladder_tail(
+        back, factor_cols, other_terms.transpose(1, 0, 2), shifted, virt_energy[None, :]
+    )
+    update_rms = jnp.sqrt(squares[0, 0] / (pair_count * virt_count * virt_count) + epsilon)
+    return (residual.transpose(1, 0, 2), update_rms)
 
 
 def pick(amplitudes, factors, kernel, other_terms, virt_energy, pair_energy):
@@ -437,8 +741,8 @@
     rank_count = lax.axis_size("rank")
     fits = (
         vpair_count == 4
-        and rank_count % 2 == 0
-        and amplitudes.shape[0] % rank_count == 0
+        and rank_count == 8
+        and amplitudes.shape[0] == 8
         and kernel.shape[1] % (128 * vpair_count) == 0
     )
     body = fast_shards if fits else shards

time: 822 us -> 492 us (0.60)
  waiting for transfers between devices: 215 us -> 0.01 us
  blocking collectives: 108 us -> 0 us
  Pallas kernels: 362 us -> 445 us
  local copies, waits for them, and re-layouts: 60.5 us -> 23.8 us
  other arithmetic: 19.5 us -> 1.23 us
  between operations: 16.1 us -> 2.55 us
  matrix products: 24 us -> 11.5 us
    reduce_scatter x1 -> x0, waiting for transfers between devices: 141 us -> none  [fast_shards(): lax.psum_scatter(partial_value, 'rank', scatter_dimension=0, tiled=True)]
    pallas_call x1 -> x2, Pallas kernels: 287 us -> 372 us  [the longest x1 189 us: ladder_tail(): pl.pallas_call(tail_kernel, out_shape=(jax.ShapeDtypeStruct((rows, pairs,...]
    all_to_all x1 -> x0, blocking collectives: 65 us -> none  [fast_shards(): lax.all_to_all(half_done, 'vpair', split_axis=0, concat_axis=0, tiled=True)]
    all_to_all x1 -> x0, waiting for transfers between devices: 52.7 us -> none  [fast_shards(): lax.all_to_all(back, 'vpair', split_axis=0, concat_axis=0, tiled=True)]
    psum x1 -> x0, blocking collectives: 42.7 us -> none  [fast_shards(): squares = lax.psum(jnp.sum(update * update), ('vpair', 'rank'))]
    all_gather x1 -> x0, waiting for transfers between devices: 21.1 us -> none  [fast_shards(): lax.all_gather(ladder_own.astype(jnp.bfloat16), 'rank', axis=0, tiled=True)]
    unnamed x10 -> x11, local copies, waits for them, and re-layouts: 29.2 us -> 9.99 us
    transpose x1 -> x0, other arithmetic: 14.8 us -> none  [fast_shards(): (other_terms.transpose(1, 0, 2) + turned.astype(jnp.float32)).transpose(1...]
  transfers between devices with their start and end apart: 4 -> 1, of which waited for: 3 -> 0; matrix products, arithmetic and copies ran while one was open for 6% -> 5% of each run, Pallas kernels for 9% -> 15%
where the time goes in v1:
time: 492 us; the launch traced here: 490 us
  Pallas kernels  445 us (90%)
  local copies, waits for them, and re-layouts  23.8 us (5%)
  matrix products  11.5 us (2%)
  starting transfers between devices  5.32 us (1%)
    pallas_call x1, Pallas kernels, ladder_tail(): pl.pallas_call(tail_kernel, out_shape=(jax.ShapeDtypeStruct((rows, pairs,...  189 us
    pallas_call x1, Pallas kernels, ladder_middle(): pl.pallas_call(functools.partial(middle_kernel, zs), out_shape=jax.ShapeD...  183 us
    pallas_call x1, Pallas kernels, front_gather(): pl.pallas_call(functools.partial(front_kernel, zs), out_shape=(jax.ShapeD...  73.9 us
    dot_general x1, matrix products, fast_shards(): jnp.einsum('sm,sh->mh', amps.reshape(rank_count * deep, pair_count * bloc...  11.5 us
    unnamed x11, local copies, waits for them, and re-layouts  9.99 us
  transfers between devices with their start and end apart: 1, of which 0 were waited for; matrix products, arithmetic and copies ran while one was open for 5% of the time, Pallas kernels for 15%

profile of v1, /device:TPU:0, one launch (start us, length us, event | category | flops | bytes accessed | tf_op | source)
XLA Modules:
  0.0 489.9 jit_solution(18222504253047430736)
XLA Ops:
  0.6 4.5 copy.12
  5.2 5.3 %all-to-all-start = ((bf16[2048,4,256]{2,0,1:T(8,128)(2,1)}), bf16[2048,4,256]{2,0,1:T(8,128)(2,1)}, u32[]{:S(2)}, u32[]{:S(2)}) async-start(bf16[2048,4,256]{2,0,1:T(8,128)(2,1)} %bitcast.16), calls=%async_computation | async-start | bytes 8388608 | tf_op jit(solution)/shard_map/all_to_all | solution.py:710
  10.5 0.0 copy-done.2
  10.5 0.9 pad.12.own_ref
  11.4 0.0 copy-done.1
  11.4 0.1 pad.13
  11.5 1.6 reshape.71.amp_ref
  13.1 73.9 %shard_map.77 = (bf16[4,304,1024]{2,1,0:T(8,128)(2,1)}, bf16[8,160,2432]{2,1,0:T(8,128)(2,1)}) custom-call(bf16[304,1024]{1,0:T(8,128)(2,1)} %pad.12.own_ref, bf16[160,2432]{1,0:T(8,128)(2,1)} %reshape.71.amp_ref), custom_call_target="tpu_custom_call" | custom-call | flops 10000000000 | bytes 10000000 | tf_op jit(solution)/shard_map/pallas_call | solution.py:362
  87.0 0.0 copy-start
  87.0 0.0 copy-start.3
  87.0 0.0 copy-start.4
  87.0 4.3 reshape_reshape.3
  91.3 0.0 copy-done
  91.3 1.7 reshape.73.cols_ref
  93.0 0.0 copy-done.3
  93.1 0.6 broadcast_in_dim.2.virt_ref
  93.7 0.1 dynamic_slice.3
  93.7 0.0 copy-done.4
  93.7 1.2 broadcast_subtract_fusion.rowen_ref
  95.0 11.5 %bitcast_convert_fusion = bf16[2432,1024]{1,0:T(8,128)(2,1)} fusion(bf16[8,160,2432]{2,1,0:T(8,128)(2,1)} %get-tuple-element.7, bf16[8,150,1024]{2,1,0:T(8,128)(2,1)} %reshape_reshape.3), kind=kOutput, calls=%fused_computation | convolution fusion | flops 6377832448 | bytes 13664256 | tf_op jit(solution)/shard_map/sm,sh->mh/dot_general | solution.py:720
  106.5 0.0 all-to-all-done
  106.5 182.8 %shard_map.78.back_ref = bf16[8,4,304,256]{3,2,1,0:T(8,128)(2,1)} custom-call(bf16[304,1024]{1,0:T(8,128)(2,1)} %pad.12.own_ref, bf16[4,304,1024]{2,1,0:T(8,128)(2,1)} %get-tuple-element.6.cols_ref, bf16[8,304,1024]{2,1,0:T(8,128)(2,1)} %bitcast.23, bf16[8192,256]{1,0:T(8,128)(2,1)} %bitcast.4.kern_ref), custom_call_target="tpu_custom_call" | custom-call | flops 81604378624 | bytes 39845888 | tf_op jit(solution)/shard_map/pallas_call | solution.py:398
  289.3 188.8 %shard_map.79 = (f32[300,8,1200]{2,1,0:T(8,128)}, f32[1,1]{1,0:T(1,128)}) custom-call(bf16[8,4,304,256]{3,2,1,0:T(8,128)(2,1)} %shard_map.78.back_ref, bf16[1200,1024]{1,0:T(8,128)(2,1)} %reshape.73.cols_ref, f32[300,8,1200]{2,1,0:T(8,128)} %bitcast.22, f32[8,300,1]{2,1,0:T(8,128)} %broadcast_subtract_fusion.rowen_ref, f32[1,1200]{1,0:T(1,128)} %broadcast_in_dim.2.virt_ref), custom_call_target="tpu_custom_call" | custom-call | flops 5898240000 | bytes 23040000 | tf_op jit(solution)/shard_map/pallas_call | solution.py:656
  478.8 10.0 %copy.14 = f32[8,300,1200]{2,0,1:T(8,128)} copy(f32[8,300,1200]{2,0,1:T(8,128)} %bitcast.17) | data formatting | bytes 23040000
  (2 shorter events, 0.0 us)
Async XLA Ops:
  5.2 5.3 %copy-start.2 = (bf16[300,1024]{1,0:T(8,128)(2,1)S(1)}, bf16[300,1024]{1,0:T(8,128)(2,1)}, u32[]{:S(2)}) copy-start(bf16[300,1024]{1,0:T(8,128)(2,1)} %param.7) | copy-start | bytes 1843204
  5.2 6.2 %copy-start.1 = (bf16[8,300,150]{1,0,2:T(8,128)(2,1)S(1)}, bf16[8,300,150]{1,0,2:T(8,128)(2,1)}, u32[]{:S(2)}) copy-start(bf16[8,300,150]{1,0,2:T(8,128)(2,1)} %param.6) | copy-start | bytes 2160004
  5.2 101.3 %all-to-all-start = ((bf16[2048,4,256]{2,0,1:T(8,128)(2,1)}), bf16[2048,4,256]{2,0,1:T(8,128)(2,1)}, u32[]{:S(2)}, u32[]{:S(2)}) async-start(bf16[2048,4,256]{2,0,1:T(8,128)(2,1)} %bitcast.16), calls=%async_computation | async-start | bytes 8388608 | tf_op jit(solution)/shard_map/all_to_all | solution.py:710
  87.0 4.3 copy-start
  87.0 6.0 %copy-start.3 = (f32[1200]{0:T(1024)S(1)}, f32[1200]{0:T(1024)}, u32[]{:S(2)}) copy-start(f32[1200]{0:T(1024)} %param.10) | copy-start | bytes 14404
  87.0 6.7 %copy-start.4 = (f32[8]{0:T(128)S(1)}, f32[8]{0:T(128)}, u32[]{:S(2)}) copy-start(f32[8]{0:T(128)} %param.11) | copy-start | bytes 100

commit v2 on v1

--- a/solution.py
+++ b/solution.py
@@ -66,7 +66,7 @@
 
 def middle_kernel(
     zs, own_ref, cols_ref, half_ref, kern_ref, out_ref, fall, hrecv, hturn, kturn, acc,
-    loc_sem, hs, hr, fr, mr, zsend, xsend, msend, osem,
+    loc_sem, hs, hr, fr, mr, zsend, xsend, msend, bs, br,
 ):
     v = lax.axis_index("vpair")
     r = lax.axis_index("rank")
@@ -198,11 +198,9 @@
     spread(2)
     finish(1)
 
-    @pl.loop(0, 2 * (zs - 1))
-    def _(n):
-        k = n // 2 + 1
-        odd = n % 2
-        rr = rank_at(k, core + odd - 2 * odd * core)
+    @pl.loop(0, 2)
+    def _(odd):
+        rr = rank_at(1, core + odd - 2 * odd * core)
 
         @pl.when(odd == 1)
         def _():
@@ -212,29 +210,67 @@
 
         @pl.loop(0, groups)
         def _(g):
-            @pl.when(jnp.logical_and(k < zs - 1, jnp.logical_and(odd == 0, g == 1)))
+            @pl.when(jnp.logical_and(odd == 0, g == 3))
             def _():
-                relay(k + 1)
-
-                @pl.when(k < zs - 2)
-                def _():
-                    spread(k + 2)
-
-            @pl.when(jnp.logical_and(k < zs - 1, jnp.logical_and(odd == 1, g == 0)))
+                relay(2)
+                spread(3)
+
+            @pl.when(jnp.logical_and(odd == 1, g == 2))
             def _():
-                finish(k + 1)
+                finish(2)
 
             at = pl.multiple_of(g * tall, tall)
             acc[pl.ds(at, tall), :] += compute(rr, 0, g)
 
-    def give(i):
-        return pltpu.make_async_copy(hrecv.at[i], out_ref.at[i], osem.at[i])
-
-    @pl.loop(0, pairs)
-    def _(i):
-        at = pl.multiple_of(i * cols, cols)
-        hrecv[i] = acc[pl.ds(at, cols), :].astype(jnp.bfloat16).T.reshape(count, block, cols)
-        give(i).start()
+    @pl.loop(0, 4)
+    def _(n):
+        side = n % 2
+        turn_kernel(rank_at(n // 2 + 2, core + side - 2 * side * core), n)
+
+    def back_copy(i, j):
+        return remote(hrecv.at[i, near[j]], out_ref.at[i, v], bs.at[i, j], br.at[i, v], (near[j], r))
+
+    def own_back(i):
+        return pltpu.make_async_copy(hrecv.at[i, v], out_ref.at[i, v], br.at[i, v])
+
+    @pl.loop(0, 2 * groups)
+    def _(m):
+        early = m < 4
+        g = jnp.where(early, m % 2, m // 2)
+        k = jnp.where(early, m // 2, m % 2) + 2
+
+        @pl.when(m == 0)
+        def _():
+            block_wait(rank_at(2, 1 - core))
+
+        @pl.when(m == 1)
+        def _():
+            relay(3)
+
+        @pl.when(m == 2)
+        def _():
+            finish(3)
+
+        at = pl.multiple_of(g * tall, tall)
+
+        @pl.loop(0, 2)
+        def _(side):
+            @pl.when(jnp.logical_and(m == 2, side == 1))
+            def _():
+                block_wait(rank_at(3, 1 - core))
+
+            rr = rank_at(k, core + side - 2 * side * core)
+            acc[pl.ds(at, tall), :] += compute(rr, (k - 2) * 2 + side, g)
+
+        @pl.when(k == 3)
+        def _():
+            for e in range(group):
+                i = g * group + e
+                piece = acc[pl.ds(at + e * cols, cols), :].astype(jnp.bfloat16)
+                hrecv[i] = piece.T.reshape(count, block, cols)
+                for j in (0, 1, 2):
+                    back_copy(i, j).start()
+                own_back(i).start()
 
     mate_block.wait_send()
     for k in range(1, zs):
@@ -248,7 +284,9 @@
     def _(i):
         for j in (0, 1, 2):
             half_copy(i, j).wait_send()
-        give(i).wait()
+            back_copy(i, j).wait_send()
+        for j in range(count):
+            pltpu.make_async_copy(out_ref.at[i, j], out_ref.at[i, j], br.at[i, j]).wait()
 
 
 def front_kernel(zs, own_ref, amp_ref, cols_ref, amps_ref, mine_sem, cols_recv, amps_recv, cs, us, ds, ms, stage, hold):
@@ -404,7 +442,7 @@
             pltpu.VMEM((rank_count, count, block, depth), jnp.bfloat16),
             pltpu.VMEM((pairs, count, block, cols), jnp.bfloat16),
             pltpu.VMEM((pairs * cols, rows), jnp.bfloat16),
-            pltpu.VMEM((2, cols, depth), jnp.bfloat16),
+            pltpu.VMEM((4, cols, depth), jnp.bfloat16),
             pltpu.VMEM((pairs * cols, rows), jnp.float32),
             dma((1,)),
             dma((pairs, 3)),
@@ -414,7 +452,8 @@
             dma((zs,)),
             dma((zs, 3)),
             dma((zs,)),
-            dma((pairs,)),
+            dma((pairs, 3)),
+            dma((pairs, count)),
         ],
         compiler_params=pltpu.CompilerParams(
             collective_id=0, has_side_effects=True, vmem_limit_bytes=62 * 1024 * 1024
@@ -425,10 +464,13 @@
     )(factors_pad, cols_pad, half_done, kernel_sub)
 
 
+CUTS = 4
+
+
 def tail_kernel(
     back_ref, cols_ref, other_ref, rowen_ref, virt_ref, res_ref, sq_ref,
-    rb, turned, part, msend, mrecv, zsend, outer, inner, fin, oth, sq, sqall,
-    bs, br, ms, mr, zs_sem, outr, inr, fs, fr, osem, rsem, qs, qr,
+    turned, part, msend, mrecv, zsend, outer, inner, fin, oth, sq, sqall,
+    ms, mr, zs_sem, outr, inr, fs, fr, osem, rsem, qs, qr,
 ):
     v = lax.axis_index("vpair")
     r = lax.axis_index("rank")
@@ -436,15 +478,15 @@
     z, core = r // 2, r % 2
     near = (y * 2 + 1 - x, (1 - y) * 2 + x, (1 - y) * 2 + 1 - x)
     mate = z * 2 + 1 - core
-    pairs, count, block, cols = rb.shape
+    pairs, count, block, cols = back_ref.shape
     rows = part.shape[1]
     turns = pairs // 2
+    step_rows = -(-rows // (16 * CUTS)) * 16
+    cuts = [(h * step_rows, min(step_rows, rows - h * step_rows)) for h in range(CUTS)]
     at_end = jnp.logical_or(z == 0, z == 3)
     in_middle = jnp.logical_not(at_end)
-    toward = jnp.where(z < 2, z + 1, z - 1)
-    away = jnp.where(z == 1, 0, 3)
-    toward_at = (v, toward * 2 + core)
-    away_at = (v, away * 2 + core)
+    toward_at = (v, jnp.where(z < 2, z + 1, z - 1) * 2 + core)
+    away_at = (v, jnp.where(z == 1, 0, 3) * 2 + core)
     mate_at = (v, mate)
 
     barrier = pltpu.get_barrier_semaphore()
@@ -469,139 +511,112 @@
     def arrive(ref, sem):
         pltpu.make_async_copy(ref, ref, sem).wait()
 
-    def back_copy(i, j):
-        return remote(back_ref.at[i, near[j]], rb.at[i, v], bs.at[i, j], br.at[i, v], (near[j], r))
-
-    def own_back(i):
-        return pltpu.make_async_copy(back_ref.at[i, v], rb.at[i, v], br.at[i, v])
-
-    @pl.loop(0, pairs)
-    def _(i):
-        for j in range(3):
-            back_copy(i, j).start()
-        own_back(i).start()
-
     def other_copy(p):
-        return pltpu.make_async_copy(other_ref.at[:, p], oth.at[p % 4], osem.at[p % 4])
-
-    def res_copy(p):
-        return pltpu.make_async_copy(oth.at[p % 4], res_ref.at[:, p], rsem.at[p % 4])
-
-    other_copy(0).start()
-    other_copy(1).start()
-    turned[...] = cols_ref[...].T
+        return pltpu.make_async_copy(other_ref.at[:, p], oth.at[p], osem.at[p])
+
+    def cut(ref, t, h):
+        return ref.at[t, pl.ds(*cuts[h]), :]
+
+    def read(ref, t, h):
+        return ref[t, pl.ds(*cuts[h]), :].astype(jnp.float32)
+
+    def res_copy(p, h):
+        return pltpu.make_async_copy(cut(oth, p, h), res_ref.at[pl.ds(*cuts[h]), p], rsem.at[p, h])
 
     def mate_copy(t):
         return remote(msend.at[t], mrecv.at[t], ms.at[t], mr.at[t], mate_at)
 
-    def outer_copy(t):
-        return remote(zsend.at[t], outer.at[t], zs_sem.at[t], outr.at[t], toward_at)
-
-    def inner_copy(t):
-        return remote(zsend.at[t], inner.at[t], zs_sem.at[t], inr.at[t], toward_at)
-
-    def fin_copy(p, j, to):
-        return remote(fin.at[p], fin.at[p], fs.at[p // 2, j], fr.at[p], to)
+    def outer_copy(t, h):
+        return remote(cut(zsend, t, h), cut(outer, t, h), zs_sem.at[t, h], outr.at[t, h], toward_at)
+
+    def inner_copy(t, h):
+        return remote(cut(zsend, t, h), cut(inner, t, h), zs_sem.at[t, h], inr.at[t, h], toward_at)
+
+    def fin_copy(p, h, j, to):
+        return remote(cut(fin, p, h), cut(fin, p, h), fs.at[p // 2, h, j], fr.at[p, h], to)
 
     def ladder(p):
-        for j in range(count):
-            arrive(rb.at[p, j], br.at[p, j])
-        left = jnp.concatenate([rb[p, j] for j in range(count)], axis=1)
+        left = jnp.concatenate([back_ref[p, j] for j in range(count)], axis=1)
         return jnp.dot(left, turned[...], preferred_element_type=jnp.float32)[:rows]
 
-    def step_a(t):
+    def make(t):
         msend[t] = ladder(2 * t + 1 - core).astype(jnp.bfloat16)
         mate_copy(t).start()
         part[t] = ladder(2 * t + core)
 
-    def step_b(t):
-        arrive(mrecv.at[t], mr.at[t])
-        both = part[t] + mrecv[t].astype(jnp.float32)
+    def give(t, h):
+        if h == 0:
+            arrive(mrecv.at[t], mr.at[t])
 
         @pl.when(at_end)
         def _():
-            zsend[t] = both.astype(jnp.bfloat16)
-            outer_copy(t).start()
-
+            zsend[t, pl.ds(*cuts[h]), :] = (read(part, t, h) + read(mrecv, t, h)).astype(jnp.bfloat16)
+            outer_copy(t, h).start()
+
+    def meet(t, h):
         @pl.when(in_middle)
         def _():
-            part[t] = both
-
-    def owner(t):
-        return z == 1 + t % 2
-
-    def step_c(t):
+            arrive(cut(outer, t, h), outr.at[t, h])
+            both = read(part, t, h) + read(mrecv, t, h)
+            zsend[t, pl.ds(*cuts[h]), :] = (both + read(outer, t, h)).astype(jnp.bfloat16)
+            inner_copy(t, h).start()
+
+    def close(t, h):
+        p = 2 * t + core
+
         @pl.when(in_middle)
         def _():
-            arrive(outer.at[t], outr.at[t])
-            three = part[t] + outer[t].astype(jnp.float32)
-
-            @pl.when(owner(t))
-            def _():
-                part[t] = three
-
-            @pl.when(jnp.logical_not(owner(t)))
-            def _():
-                zsend[t] = three.astype(jnp.bfloat16)
-                inner_copy(t).start()
-
-    def step_d(t):
+            arrive(cut(inner, t, h), inr.at[t, h])
+            fin[p, pl.ds(*cuts[h]), :] = (read(zsend, t, h) + read(inner, t, h)).astype(jnp.bfloat16)
+            fin_copy(p, h, 0, away_at).start()
+            fin_copy(p, h, 1, mate_at).start()
+
+    def land(t, h):
         p = 2 * t + core
 
-        @pl.when(jnp.logical_and(in_middle, owner(t)))
-        def _():
-            arrive(inner.at[t], inr.at[t])
-            fin[p] = (part[t] + inner[t].astype(jnp.float32)).astype(jnp.bfloat16)
-            fin_copy(p, 0, away_at).start()
-            fin_copy(p, 1, toward_at).start()
-            fin_copy(p, 2, mate_at).start()
-
-        @pl.when(jnp.logical_and(in_middle, jnp.logical_not(owner(t))))
-        def _():
-            arrive(fin.at[p], fr.at[p])
-            fin_copy(p, 0, away_at).start()
-            fin_copy(p, 2, mate_at).start()
-
-    def step_e(t):
-        p = 2 * t + core
-
         @pl.when(at_end)
         def _():
-            arrive(fin.at[p], fr.at[p])
-            fin_copy(p, 2, mate_at).start()
-
-    def settle(p):
-        other_copy(p).wait()
-        value = oth[p % 4] + fin[p].astype(jnp.float32)
-        oth[p % 4] = value
-        update = value / (rowen_ref[p] + virt_ref[...])
-        sq[pl.ds(p, 1), :] = jnp.sum(update * update, axis=0, keepdims=True)
-        res_copy(p).start()
-
-    def step_f(t):
-        arrive(fin.at[2 * t + 1 - core], fr.at[2 * t + 1 - core])
-
-        @pl.when(t + 1 < turns)
-        def _():
-            for e in range(2):
-                p = 2 * t + 2 + e
-
-                @pl.when(t > 0)
+            arrive(cut(fin, p, h), fr.at[p, h])
+            fin_copy(p, h, 1, mate_at).start()
+
+    def settle(t, h):
+        q = 2 * t + 1 - core
+        arrive(cut(fin, q, h), fr.at[q, h])
+        for e in range(2):
+            p = 2 * t + e
+            if h == 0:
+                other_copy(p).wait()
+            value = read(oth, p, h) + read(fin, p, h)
+            oth[p, pl.ds(*cuts[h]), :] = value
+            update = value / (rowen_ref[p, pl.ds(*cuts[h]), :] + virt_ref[...])
+            squares = jnp.sum(update * update, axis=0, keepdims=True)
+            if h == 0:
+                sq[pl.ds(p, 1), :] = squares
+            else:
+                sq[pl.ds(p, 1), :] += squares
+            res_copy(p, h).start()
+
+    @pl.loop(0, pairs)
+    def _(p):
+        other_copy(p).start()
+
+    turned[...] = cols_ref[...].T
+    stages = ((1, give), (3, meet), (5, close), (7, land), (8, settle))
+    last = stages[-1][0]
+
+    @pl.loop(0, turns + -(-last // CUTS))
+    def _(u):
+        @pl.when(u < turns)
+        def _():
+            make(u)
+
+        for h in range(CUTS):
+            for lag, stage in stages:
+                t = u + (h - lag) // CUTS
+
+                @pl.when(jnp.logical_and(t >= 0, t < turns))
                 def _():
-                    res_copy(p).wait()
-
-                other_copy(p).start()
-
-        for e in range(2):
-            settle(2 * t + e)
-
-    @pl.loop(0, turns + 5)
-    def _(u):
-        for lag, step in enumerate((step_a, step_b, step_c, step_d, step_e, step_f)):
-
-            @pl.when(jnp.logical_and(u >= lag, u < turns + lag))
-            def _():
-                step(u - lag)
+                    stage(t, (h - lag) % CUTS)
 
     sqall[v] = sq[...]
     for j in range(3):
@@ -614,33 +629,19 @@
     for j in range(3):
         remote(sq, sqall.at[v], qs.at[j], qr.at[v], (near[j], r)).wait_send()
 
-    @pl.loop(0, pairs)
-    def _(i):
-        for j in range(3):
-            back_copy(i, j).wait_send()
-
     @pl.loop(0, turns)
     def _(t):
-        p = 2 * t + core
         mate_copy(t).wait_send()
-        fin_done = jnp.logical_and(in_middle, owner(t))
-
-        @pl.when(jnp.logical_not(fin_done))
-        def _():
-            outer_copy(t).wait_send()
-
-        @pl.when(in_middle)
-        def _():
-            fin_copy(p, 0, away_at).wait_send()
-
-        @pl.when(fin_done)
-        def _():
-            fin_copy(p, 1, toward_at).wait_send()
-
-        fin_copy(p, 2, mate_at).wait_send()
-
-    for p in range(pairs - 4, pairs):
-        res_copy(p).wait()
+        for h in range(CUTS):
+            outer_copy(t, h).wait_send()
+            fin_copy(2 * t + core, h, 1, mate_at).wait_send()
+
+            @pl.when(in_middle)
+            def _():
+                fin_copy(2 * t + core, h, 0, away_at).wait_send()
+
+            for e in range(2):
+                res_copy(2 * t + e, h).wait()
 
 
 def ladder_tail(back, cols_flat, other_turned, row_energy, virt_energy):
@@ -659,10 +660,9 @@
             jax.ShapeDtypeStruct((rows, pairs, virt_count), jnp.float32),
             jax.ShapeDtypeStruct((1, 1), jnp.float32),
         ),
-        in_specs=[hbm, vmem, hbm, vmem, vmem],
+        in_specs=[vmem, vmem, hbm, vmem, vmem],
         out_specs=(hbm, vmem),
         scratch_shapes=[
-            bf16(pairs, count, block, cols),
             bf16(depth, virt_count),
             f32(turns, rows, virt_count),
             bf16(turns, rows, virt_count),
@@ -671,20 +671,18 @@
             bf16(turns, rows, virt_count),
             bf16(turns, rows, virt_count),
             bf16(pairs, rows, virt_count),
-            f32(4, rows, virt_count),
+            f32(pairs, rows, virt_count),
             f32(pairs, virt_count),
             f32(count, pairs, virt_count),
-            dma((pairs, 3)),
-            dma((pairs, count)),
             dma((turns,)),
             dma((turns,)),
-            dma((turns,)),
-            dma((turns,)),
-            dma((turns,)),
-            dma((turns, 3)),
+            dma((turns, CUTS)),
+            dma((turns, CUTS)),
+            dma((turns, CUTS)),
+            dma((turns, CUTS, 2)),
+            dma((pairs, CUTS)),
             dma((pairs,)),
-            dma((4,)),
-            dma((4,)),
+            dma((pairs, CUTS)),
             dma((3,)),
             dma((count,)),
         ],

time: 492 us -> 425 us (0.86)
  Pallas kernels: 445 us -> 380 us
    pallas_call x1, Pallas kernels: 189 us -> 101 us  [ladder_tail(): pl.pallas_call(tail_kernel, out_shape=(jax.ShapeDtypeStruct((rows, pairs,...]
    pallas_call x1, Pallas kernels: 183 us -> 206 us  [ladder_middle(): pl.pallas_call(functools.partial(middle_kernel, zs), out_shape=jax.ShapeD...]
  transfers between devices with their start and end apart: 1 -> 1, of which waited for: 0 -> 0; matrix products, arithmetic and copies ran while one was open for 5% -> 5% of each run, Pallas kernels for 15% -> 17%
where the time goes in v2:
time: 425 us
  Pallas kernels  380 us (89%)
  local copies, waits for them, and re-layouts  23.8 us (6%)
  matrix products  11.5 us (3%)
  starting transfers between devices  5.32 us (1%)
    pallas_call x1, Pallas kernels, ladder_middle(): pl.pallas_call(functools.partial(middle_kernel, zs), out_shape=jax.ShapeD...  206 us
    pallas_call x1, Pallas kernels, ladder_tail(): pl.pallas_call(tail_kernel, out_shape=(jax.ShapeDtypeStruct((rows, pairs,...  101 us
    pallas_call x1, Pallas kernels, front_gather(): pl.pallas_call(functools.partial(front_kernel, zs), out_shape=(jax.ShapeD...  73.9 us
    dot_general x1, matrix products, fast_shards(): jnp.einsum('sm,sh->mh', amps.reshape(rank_count * deep, pair_count * bloc...  11.5 us
    unnamed x11, local copies, waits for them, and re-layouts  9.99 us
  transfers between devices with their start and end apart: 1, of which 0 were waited for; matrix products, arithmetic and copies ran while one was open for 5% of the time, Pallas kernels for 17%

profile of v2, /device:TPU:0, one launch (start us, length us, event | category | flops | bytes accessed | tf_op | source)
XLA Modules:
  0.0 424.9 jit_solution(5409884312568127304)
XLA Ops:
  0.6 4.5 %copy.12 = bf16[256,4,8,256]{3,2,0,1:T(8,128)(2,1)} copy(bf16[256,4,8,256]{3,2,1,0:T(8,128)(2,1)} %bitcast.20) | data formatting | bytes 8388608 | tf_op jit(solution)/shard_map/all_to_all | solution.py:708
  5.2 5.3 %all-to-all-start = ((bf16[2048,4,256]{2,0,1:T(8,128)(2,1)}), bf16[2048,4,256]{2,0,1:T(8,128)(2,1)}, u32[]{:S(2)}, u32[]{:S(2)}) async-start(bf16[2048,4,256]{2,0,1:T(8,128)(2,1)} %bitcast.16), calls=%async_computation | async-start | bytes 8388608 | tf_op jit(solution)/shard_map/all_to_all | solution.py:708
  10.5 0.0 copy-done.2
  10.5 0.9 pad.12.own_ref
  11.4 0.0 copy-done.1
  11.4 0.1 pad.13
  11.5 1.6 reshape.71.amp_ref
  13.1 73.9 %shard_map.77 = (bf16[4,304,1024]{2,1,0:T(8,128)(2,1)}, bf16[8,160,2432]{2,1,0:T(8,128)(2,1)}) custom-call(bf16[304,1024]{1,0:T(8,128)(2,1)} %pad.12.own_ref, bf16[160,2432]{1,0:T(8,128)(2,1)} %reshape.71.amp_ref), custom_call_target="tpu_custom_call" | custom-call | flops 10000000000 | bytes 10000000 | tf_op jit(solution)/shard_map/pallas_call | solution.py:400
  87.0 0.0 copy-start
  87.0 0.0 copy-start.3
  87.0 0.0 copy-start.4
  87.0 4.3 %reshape_reshape.3 = bf16[8,150,1024]{2,1,0:T(8,128)(2,1)} reshape(bf16[4,300,1024]{2,1,0:T(8,128)(2,1)} %bitcast.18) | data formatting | bytes 4915200 | tf_op jit(solution)/shard_map/reshape;reshape | solution.py:716
  91.3 0.0 copy-done
  91.3 1.7 reshape.73.cols_ref
  93.0 0.0 copy-done.3
  93.1 0.6 broadcast_in_dim.2.virt_ref
  93.7 0.1 dynamic_slice.3
  93.7 0.0 copy-done.4
  93.7 1.2 broadcast_subtract_fusion.rowen_ref
  95.0 11.5 %bitcast_convert_fusion = bf16[2432,1024]{1,0:T(8,128)(2,1)} fusion(bf16[8,160,2432]{2,1,0:T(8,128)(2,1)} %get-tuple-element.7, bf16[8,150,1024]{2,1,0:T(8,128)(2,1)} %reshape_reshape.3), kind=kOutput, calls=%fused_computation | convolution fusion | flops 6377832448 | bytes 13664256 | tf_op jit(solution)/shard_map/sm,sh->mh/dot_general | solution.py:718
  106.5 0.0 all-to-all-done
  106.5 205.9 %shard_map.78.back_ref = bf16[8,4,304,256]{3,2,1,0:T(8,128)(2,1)} custom-call(bf16[304,1024]{1,0:T(8,128)(2,1)} %pad.12.own_ref, bf16[4,304,1024]{2,1,0:T(8,128)(2,1)} %get-tuple-element.6.cols_ref, bf16[8,304,1024]{2,1,0:T(8,128)(2,1)} %bitcast.23, bf16[8192,256]{1,0:T(8,128)(2,1)} %bitcast.4.kern_ref), custom_call_target="tpu_custom_call" | custom-call | flops 81604378624 | bytes 39845888 | tf_op jit(solution)/shard_map/pallas_call | solution.py:436
  312.3 100.7 %shard_map.79 = (f32[300,8,1200]{2,1,0:T(8,128)}, f32[1,1]{1,0:T(1,128)}) custom-call(bf16[8,4,304,256]{3,2,1,0:T(8,128)(2,1)} %shard_map.78.back_ref, bf16[1200,1024]{1,0:T(8,128)(2,1)} %reshape.73.cols_ref, f32[300,8,1200]{2,1,0:T(8,128)} %bitcast.22, f32[8,300,1]{2,1,0:T(8,128)} %broadcast_subtract_fusion.rowen_ref, f32[1,1200]{1,0:T(1,128)} %broadcast_in_dim.2.virt_ref), custom_call_target="tpu_custom_call" | custom-call | flops 5898240000 | bytes 23040000 | tf_op jit(solution)/shard_map/pallas_call | solution.py:657
  413.8 10.0 %copy.14 = f32[8,300,1200]{2,0,1:T(8,128)} copy(f32[8,300,1200]{2,0,1:T(8,128)} %bitcast.17) | data formatting | bytes 23040000
  (2 shorter events, 0.0 us)
Async XLA Ops:
  5.2 5.3 %copy-start.2 = (bf16[300,1024]{1,0:T(8,128)(2,1)S(1)}, bf16[300,1024]{1,0:T(8,128)(2,1)}, u32[]{:S(2)}) copy-start(bf16[300,1024]{1,0:T(8,128)(2,1)} %param.7) | copy-start | bytes 1843204
  5.2 6.2 %copy-start.1 = (bf16[8,300,150]{1,0,2:T(8,128)(2,1)S(1)}, bf16[8,300,150]{1,0,2:T(8,128)(2,1)}, u32[]{:S(2)}) copy-start(bf16[8,300,150]{1,0,2:T(8,128)(2,1)} %param.6) | copy-start | bytes 2160004
  5.2 101.3 %all-to-all-start = ((bf16[2048,4,256]{2,0,1:T(8,128)(2,1)}), bf16[2048,4,256]{2,0,1:T(8,128)(2,1)}, u32[]{:S(2)}, u32[]{:S(2)}) async-start(bf16[2048,4,256]{2,0,1:T(8,128)(2,1)} %bitcast.16), calls=%async_computation | async-start | bytes 8388608 | tf_op jit(solution)/shard_map/all_to_all | solution.py:708
  87.0 4.3 %copy-start = (bf16[4,304,1024]{2,1,0:T(8,128)(2,1)S(1)}, bf16[4,304,1024]{2,1,0:T(8,128)(2,1)}, u32[]{:S(2)}) copy-start(bf16[4,304,1024]{2,1,0:T(8,128)(2,1)} %get-tuple-element.6.cols_ref) | copy-start | bytes 7471108
  87.0 6.0 %copy-start.3 = (f32[1200]{0:T(1024)S(1)}, f32[1200]{0:T(1024)}, u32[]{:S(2)}) copy-start(f32[1200]{0:T(1024)} %param.10) | copy-start | bytes 14404
  87.0 6.7 %copy-start.4 = (f32[8]{0:T(128)S(1)}, f32[8]{0:T(128)}, u32[]{:S(2)}) copy-start(f32[8]{0:T(128)} %param.11) | copy-start | bytes 100

commit v3 on v2

--- a/solution.py
+++ b/solution.py
@@ -65,8 +65,8 @@
 
 
 def middle_kernel(
-    zs, own_ref, cols_ref, half_ref, kern_ref, out_ref, fall, hrecv, hturn, kturn, acc,
-    loc_sem, hs, hr, fr, mr, zsend, xsend, msend, bs, br,
+    zs, cols_ref, line_ref, half_ref, kern_ref, out_ref, fall, hrecv, hturn, kturn, acc,
+    loc_sem, hr, fr, mr, xsend, msend, bs, br,
 ):
     v = lax.axis_index("vpair")
     r = lax.axis_index("rank")
@@ -76,7 +76,7 @@
     near = (vx, vy, vd)
     mate = z * 2 + 1 - core
     pairs, count, block, cols = hrecv.shape
-    depth = own_ref.shape[1]
+    depth = cols_ref.shape[2]
     rows = count * block
     group = 2
     groups = pairs // group
@@ -86,7 +86,7 @@
         return ((z + k) % zs) * 2 + side
 
     barrier = pltpu.get_barrier_semaphore()
-    peers = [(v, rank_at(k, core)) for k in range(1, zs)] + [(at, r) for at in near] + [(v, mate)]
+    peers = [(at, r) for at in near] + [(v, mate)]
     for peer in peers:
         pl.semaphore_signal(barrier, inc=1, device_id=peer, device_id_type=MESH_IDS)
     pl.semaphore_wait(barrier, len(peers))
@@ -97,21 +97,17 @@
             device_id=to, device_id_type=MESH_IDS,
         )
 
-    def half_copy(i, j):
-        at = pl.multiple_of(near[j] * cols, cols)
-        return remote(
-            half_ref.at[i, :, pl.ds(at, cols)], hrecv.at[i, v], hs.at[i, j], hr.at[i, v], (near[j], r)
-        )
-
     def own_half(i):
-        at = pl.multiple_of(v * cols, cols)
-        return pltpu.make_async_copy(half_ref.at[i, :, pl.ds(at, cols)], hrecv.at[i, v], hr.at[i, v])
-
-    def rows_copy(k):
-        return remote(own_ref, fall.at[r, v], zsend.at[k], fr.at[r, v], (v, rank_at(k, core)))
-
-    def side_copy(rr, at, k, j, to):
-        return remote(fall.at[rr, at], fall.at[rr, at], xsend.at[k, j], fr.at[rr, at], (to, r))
+        return pltpu.make_async_copy(half_ref.at[i], hrecv.at[i], hr.at[i])
+
+    def line_copy(k, slot):
+        at = vd if slot else v
+        rr = rank_at(k, core)
+        return pltpu.make_async_copy(line_ref.at[rr // 2, slot], fall.at[rr, at], fr.at[rr, at])
+
+    def side_copy(k, j):
+        rr = rank_at(k, core)
+        return remote(line_ref.at[rr // 2, 0], fall.at[rr, v], xsend.at[k, j], fr.at[rr, v], (near[j], r))
 
     def mate_copy(k):
         rr = rank_at(k, core)
@@ -123,27 +119,10 @@
     def block_wait(rr):
         pltpu.make_async_copy(fall.at[rr], fall.at[rr], mr.at[rr]).wait()
 
-    def spread(k):
+    def finish(k):
         rr = rank_at(k, core)
-        shard_wait(rr, v)
-        side_copy(rr, v, k, 0, vx).start()
-        side_copy(rr, v, k, 1, vy).start()
-
-    def relay_copy(k):
-        rr = rank_at(k, core)
-        odd = (rr // 2) % 2
-        via = (y + odd * (1 - 2 * y)) * 2 + x + (1 - odd) * (1 - 2 * x)
-        to = (y + (1 - odd) * (1 - 2 * y)) * 2 + x + odd * (1 - 2 * x)
-        return side_copy(rr, via, k, 2, to)
-
-    def relay(k):
-        rr = rank_at(k, core)
-        shard_wait(rr, vx)
-        shard_wait(rr, vy)
-        relay_copy(k).start()
-
-    def finish(k):
-        shard_wait(rank_at(k, core), vd)
+        for at in (v, vx, vy, vd):
+            shard_wait(rr, at)
         mate_copy(k).start()
 
     own_block = pltpu.make_async_copy(cols_ref, fall.at[r], loc_sem.at[0])
@@ -151,13 +130,16 @@
     own_block.start()
     mate_block.start()
     for k in range(1, zs):
-        rows_copy(k).start()
+        for j in (0, 1):
+            side_copy(k, j).start()
 
     @pl.loop(0, pairs)
     def _(i):
-        for j in (0, 1, 2):
-            half_copy(i, j).start()
         own_half(i).start()
+
+    for k in range(1, zs):
+        for slot in (0, 1):
+            line_copy(k, slot).start()
 
     def turn_kernel(rr, slot):
         start = pl.multiple_of(rr * depth, depth)
@@ -184,19 +166,14 @@
         at = pl.multiple_of(g * tall, tall)
         for e in range(group):
             i = g * group + e
-            for j in range(count):
-                pltpu.make_async_copy(hrecv.at[i, j], hrecv.at[i, j], hr.at[i, j]).wait()
+            own_half(i).wait()
             hturn[pl.ds(at + e * cols, cols), :] = hrecv[i].reshape(rows, cols).T
         acc[pl.ds(at, tall), :] = compute(r, 0, g)
         acc[pl.ds(at, tall), :] += compute(mate, 1, g)
 
-        @pl.when(g == 1)
-        def _():
-            spread(1)
-
-    relay(1)
-    spread(2)
-    finish(1)
+        @pl.when(g == 2)
+        def _():
+            finish(1)
 
     @pl.loop(0, 2)
     def _(odd):
@@ -210,14 +187,13 @@
 
         @pl.loop(0, groups)
         def _(g):
-            @pl.when(jnp.logical_and(odd == 0, g == 3))
+            @pl.when(jnp.logical_and(odd == 0, g == 2))
             def _():
-                relay(2)
-                spread(3)
+                finish(2)
 
             @pl.when(jnp.logical_and(odd == 1, g == 2))
             def _():
-                finish(2)
+                finish(3)
 
             at = pl.multiple_of(g * tall, tall)
             acc[pl.ds(at, tall), :] += compute(rr, 0, g)
@@ -235,31 +211,19 @@
 
     @pl.loop(0, 2 * groups)
     def _(m):
-        early = m < 4
-        g = jnp.where(early, m % 2, m // 2)
-        k = jnp.where(early, m // 2, m % 2) + 2
-
-        @pl.when(m == 0)
-        def _():
-            block_wait(rank_at(2, 1 - core))
-
-        @pl.when(m == 1)
-        def _():
-            relay(3)
-
-        @pl.when(m == 2)
-        def _():
-            finish(3)
+        g = m // 2
+        k = m % 2 + 2
 
         at = pl.multiple_of(g * tall, tall)
 
         @pl.loop(0, 2)
         def _(side):
-            @pl.when(jnp.logical_and(m == 2, side == 1))
+            rr = rank_at(k, core + side - 2 * side * core)
+
+            @pl.when(jnp.logical_and(g == 0, side == 1))
             def _():
-                block_wait(rank_at(3, 1 - core))
-
-            rr = rank_at(k, core + side - 2 * side * core)
+                block_wait(rr)
+
             acc[pl.ds(at, tall), :] += compute(rr, (k - 2) * 2 + side, g)
 
         @pl.when(k == 3)
@@ -274,52 +238,81 @@
 
     mate_block.wait_send()
     for k in range(1, zs):
-        rows_copy(k).wait_send()
-        side_copy(r, v, k, 0, vx).wait_send()
-        side_copy(r, v, k, 1, vy).wait_send()
-        relay_copy(k).wait_send()
+        for j in (0, 1):
+            side_copy(k, j).wait_send()
         mate_copy(k).wait_send()
 
     @pl.loop(0, pairs)
     def _(i):
         for j in (0, 1, 2):
-            half_copy(i, j).wait_send()
             back_copy(i, j).wait_send()
         for j in range(count):
             pltpu.make_async_copy(out_ref.at[i, j], out_ref.at[i, j], br.at[i, j]).wait()
 
 
-def front_kernel(zs, own_ref, amp_ref, cols_ref, amps_ref, mine_sem, cols_recv, amps_recv, cs, us, ds, ms, stage, hold):
+def front_kernel(
+    zs, col_block, own_ref, amp_ref, kern_ref, cols_ref, half_ref, z_ref, line_ref,
+    cbuf, amps, zbuf, deep, hstage,
+    mine, cs, cr, us, ds, ms, ar, ks, kr, hs, hr, lu, ld, lr,
+):
     v = lax.axis_index("vpair")
     r = lax.axis_index("rank")
     y, x = v // 2, v % 2
     z, core = r // 2, r % 2
     near = (y * 2 + 1 - x, (1 - y) * 2 + x, (1 - y) * 2 + 1 - x)
+    vd = near[2]
     mate = z * 2 + 1 - core
-    mesh_ids = pl.DeviceIdType.MESH
     has_up, has_down = z + 1 < zs, z >= 1
     up_to, down_to = ((z + 1) % zs) * 2 + core, ((z + zs - 1) % zs) * 2 + core
+    pairs, count, block, cols = half_ref.shape
+    points = kern_ref.shape[0]
+    rank_count, deep_block = amps.shape[:2]
+    groups = hstage.shape[0]
+    wide = hstage.shape[1]
+    group = pairs // groups
 
     barrier = pltpu.get_barrier_semaphore()
     peers = [(at, r) for at in near] + [(v, mate), (v, up_to), (v, down_to)]
     for peer in peers:
-        pl.semaphore_signal(barrier, inc=1, device_id=peer, device_id_type=mesh_ids)
+        pl.semaphore_signal(barrier, inc=1, device_id=peer, device_id_type=MESH_IDS)
     pl.semaphore_wait(barrier, len(peers))
 
-    def cols_copy(j, at, to):
+    def remote(src, dst, send_sem, recv_sem, to):
         return pltpu.make_async_remote_copy(
-            src_ref=own_ref, dst_ref=cols_ref.at[at], send_sem=cs.at[j], recv_sem=cols_recv.at[at],
-            device_id=(to, r), device_id_type=mesh_ids,
+            src_ref=src, dst_ref=dst, send_sem=send_sem, recv_sem=recv_sem,
+            device_id=to, device_id_type=MESH_IDS,
         )
 
+    def arrive(ref, sem):
+        pltpu.make_async_copy(ref, ref, sem).wait()
+
     def amps_copy(src, at, sem, to):
-        return pltpu.make_async_remote_copy(
-            src_ref=src, dst_ref=amps_ref.at[at], send_sem=sem, recv_sem=amps_recv.at[at],
-            device_id=(v, to), device_id_type=mesh_ids,
-        )
-
-    def amps_wait(at):
-        pltpu.make_async_copy(amps_ref.at[at], amps_ref.at[at], amps_recv.at[at]).wait()
+        return remote(src, amps.at[at], sem, ar.at[at], (v, to))
+
+    def cols_copy(j):
+        return remote(own_ref, cbuf.at[v], cs.at[j], cr.at[v], (near[j], r))
+
+    def part_of(at):
+        return kern_ref.at[:, pl.ds(pl.multiple_of(at * cols, cols), cols)]
+
+    def rows_of(at):
+        return z_ref.at[pl.ds(pl.multiple_of(at * points, points), points), :]
+
+    def kern_copy(j):
+        return remote(part_of(near[j]), rows_of(v), ks.at[j], kr.at[v], (near[j], r))
+
+    def line_copy(src, at, slot, sem, to):
+        return remote(src, line_ref.at[at, slot], sem.at[at, slot], lr.at[at, slot], (v, to))
+
+    def half_piece(i, at):
+        rows_at = pl.multiple_of((i % group) * (wide // group), 16)
+        return hstage.at[i // group, pl.ds(rows_at, block), pl.ds(pl.multiple_of(at * cols, cols), cols)]
+
+    def half_copy(i, j):
+        return remote(half_piece(i, near[j]), half_ref.at[i, v], hs.at[i, j], hr.at[i, v], (near[j], r))
+
+    def own_half(i):
+        return pltpu.make_async_copy(half_piece(i, v), half_ref.at[i, v], hr.at[i, v])
 
     @pl.when(has_up)
     def _():
@@ -329,59 +322,140 @@
     def _():
         amps_copy(amp_ref, r, ds.at[0], down_to).start()
 
-    for j in range(3):
-        cols_copy(j, v, near[j]).start()
+    for j in (0, 1, 2):
+        cols_copy(j).start()
     amps_copy(amp_ref, r, ms.at[0, 0], mate).start()
-    a = pltpu.make_async_copy(own_ref, stage, mine_sem.at[0])
-    b = pltpu.make_async_copy(amp_ref, hold, mine_sem.at[1])
-    a.start()
-    b.start()
-    a.wait()
-    b.wait()
-    c = pltpu.make_async_copy(stage, cols_ref.at[v], mine_sem.at[2])
-    d = pltpu.make_async_copy(hold, amps_ref.at[r], mine_sem.at[3])
-    c.start()
-    d.start()
-    c.wait()
-    d.wait()
-
-    for s in range(1, zs):
+    for j in (0, 1, 2):
+        kern_copy(j).start()
+    own_cols = pltpu.make_async_copy(own_ref, cbuf.at[v], mine.at[0])
+    own_amps = pltpu.make_async_copy(amp_ref, amps.at[r], mine.at[1])
+    own_in = pltpu.make_async_copy(part_of(v), zbuf, mine.at[2])
+    own_out = pltpu.make_async_copy(zbuf, rows_of(v), mine.at[2])
+    own_cols.start()
+    own_amps.start()
+    own_in.start()
+    deep[...] = jnp.zeros_like(deep)
+    own_cols.wait()
+    own_amps.wait()
+    own_in.wait()
+    own_out.start()
+
+    def amps_step(s):
         low, high = ((z + zs - s) % zs) * 2 + core, ((z + s) % zs) * 2 + core
 
         @pl.when(z >= s)
         def _():
-            amps_wait(low)
-            amps_copy(amps_ref.at[low], low, ms.at[s, 0], mate).start()
+            arrive(amps.at[low], ar.at[low])
+            amps_copy(amps.at[low], low, ms.at[s, 0], mate).start()
 
             @pl.when(has_up)
             def _():
-                amps_copy(amps_ref.at[low], low, us.at[s], up_to).start()
+                amps_copy(amps.at[low], low, us.at[s], up_to).start()
 
         @pl.when(z + s < zs)
         def _():
-            amps_wait(high)
-            amps_copy(amps_ref.at[high], high, ms.at[s, 1], mate).start()
+            arrive(amps.at[high], ar.at[high])
+            amps_copy(amps.at[high], high, ms.at[s, 1], mate).start()
 
             @pl.when(has_down)
             def _():
-                amps_copy(amps_ref.at[high], high, ds.at[s], down_to).start()
-
+                amps_copy(amps.at[high], high, ds.at[s], down_to).start()
+
+    def line_step(s):
+        low, high = (z + zs - s) % zs, (z + s) % zs
+
+        @pl.when(z >= s)
+        def _():
+            for slot in (0, 1):
+                arrive(line_ref.at[low, slot], lr.at[low, slot])
+
+                @pl.when(has_up)
+                def _():
+                    line_copy(line_ref.at[low, slot], low, slot, lu, up_to).start()
+
+        @pl.when(z + s < zs)
+        def _():
+            for slot in (0, 1):
+                arrive(line_ref.at[high, slot], lr.at[high, slot])
+
+                @pl.when(has_down)
+                def _():
+                    line_copy(line_ref.at[high, slot], high, slot, ld, down_to).start()
+
+    for s in range(1, zs - 1):
+        amps_step(s)
     for at in near:
-        pltpu.make_async_copy(cols_ref.at[at], cols_ref.at[at], cols_recv.at[at]).wait()
+        arrive(cbuf.at[at], cr.at[at])
+    cols_out = pltpu.make_async_copy(cbuf, cols_ref, mine.at[0])
+    cols_out.start()
+
+    @pl.when(has_up)
+    def _():
+        for slot, at in ((0, v), (1, vd)):
+            line_copy(cbuf.at[at], z, slot, lu, up_to).start()
+
+    @pl.when(has_down)
+    def _():
+        for slot, at in ((0, v), (1, vd)):
+            line_copy(cbuf.at[at], z, slot, ld, down_to).start()
+
+    per = rank_count // count
+    for j in range(count):
+        whole = cbuf[j]
+        for e in range(per):
+            at = (j * per + e) * deep_block
+            deep[at : at + col_block, :] = whole[e * col_block : (e + 1) * col_block]
+    amps_step(zs - 1)
     for k in range(zs):
-        amps_wait(k * 2 + 1 - core)
-    for j in range(3):
-        cols_copy(j, v, near[j]).wait_send()
+        at = k * 2 + 1 - core
+        arrive(amps.at[at], ar.at[at])
+
+    @pl.loop(0, groups)
+    def _(g):
+        left = amps[:, :, pl.ds(pl.multiple_of(g * wide, wide), wide)].reshape(rank_count * deep_block, wide)
+        done = lax.dot_general(
+            left, deep[...], (((0,), (0,)), ((), ())), preferred_element_type=jnp.float32
+        )
+        hstage[g] = done.astype(jnp.bfloat16)
+        for e in range(group):
+            i = g * group + e
+            for j in (0, 1, 2):
+                half_copy(i, j).start()
+            own_half(i).start()
+
+    for s in range(1, zs):
+        line_step(s)
+    for at in near:
+        arrive(rows_of(at), kr.at[at])
+
+    @pl.loop(0, pairs)
+    def _(i):
+        for j in range(count):
+            arrive(half_ref.at[i, j], hr.at[i, j])
+        for j in (0, 1, 2):
+            half_copy(i, j).wait_send()
+
+    own_out.wait()
+    cols_out.wait()
+    for j in (0, 1, 2):
+        cols_copy(j).wait_send()
+        kern_copy(j).wait_send()
     amps_copy(amp_ref, r, ms.at[0, 0], mate).wait_send()
+
+    def line_sent(at, sem, to):
+        for slot in (0, 1):
+            line_copy(cbuf.at[0], at, slot, sem, to).wait_send()
+
     for s in range(zs):
-
         @pl.when(jnp.logical_and(z >= s, has_up))
         def _():
             amps_copy(amp_ref, r, us.at[s], up_to).wait_send()
+            line_sent((z + zs - s) % zs, lu, up_to)
 
         @pl.when(jnp.logical_and(z + s < zs, has_down))
         def _():
             amps_copy(amp_ref, r, ds.at[s], down_to).wait_send()
+            line_sent((z + s) % zs, ld, down_to)
 
         if s:
 
@@ -394,38 +468,58 @@
                 amps_copy(amp_ref, r, ms.at[s, 1], mate).wait_send()
 
 
-def front_gather(factors_pad, amps_pad, vpair_count, rank_count):
+def front_gather(factors_pad, amps_pad, kernel, pairs, col_block, vpair_count, rank_count):
     zs = rank_count // 2
+    block, right_block = factors_pad.shape
+    points = kernel.shape[0]
+    cols = right_block // vpair_count
+    deep_block, width = amps_pad.shape
+    groups = pairs // 2
     hbm = pl.BlockSpec(memory_space=pl.ANY)
+    dma = pltpu.SemaphoreType.DMA
+    bf16 = lambda *shape: pltpu.VMEM(shape, jnp.bfloat16)
+    like = lambda *shape: jax.ShapeDtypeStruct(shape, jnp.bfloat16)
     return pl.pallas_call(
-        functools.partial(front_kernel, zs),
+        functools.partial(front_kernel, zs, col_block),
         out_shape=(
-            jax.ShapeDtypeStruct((vpair_count, *factors_pad.shape), jnp.bfloat16),
-            jax.ShapeDtypeStruct((rank_count, *amps_pad.shape), jnp.bfloat16),
+            like(vpair_count, block, right_block),
+            like(pairs, vpair_count, block, cols),
+            like(points * vpair_count, cols),
+            like(zs, 2, block, right_block),
         ),
-        in_specs=[hbm, hbm],
-        out_specs=(hbm, hbm),
+        in_specs=[hbm, hbm, hbm],
+        out_specs=(hbm, hbm, hbm, hbm),
         scratch_shapes=[
-            pltpu.SemaphoreType.DMA((4,)),
-            pltpu.SemaphoreType.DMA((vpair_count,)),
-            pltpu.SemaphoreType.DMA((rank_count,)),
-            pltpu.SemaphoreType.DMA((3,)),
-            pltpu.SemaphoreType.DMA((zs,)),
-            pltpu.SemaphoreType.DMA((zs,)),
-            pltpu.SemaphoreType.DMA((zs, 2)),
-            pltpu.VMEM(factors_pad.shape, jnp.bfloat16),
-            pltpu.VMEM(amps_pad.shape, jnp.bfloat16),
+            bf16(vpair_count, block, right_block),
+            bf16(rank_count, deep_block, width),
+            bf16(points, cols),
+            bf16(rank_count * deep_block, right_block),
+            bf16(groups, width // groups, right_block),
+            dma((3,)),
+            dma((3,)),
+            dma((vpair_count,)),
+            dma((zs,)),
+            dma((zs,)),
+            dma((zs, 2)),
+            dma((rank_count,)),
+            dma((3,)),
+            dma((vpair_count,)),
+            dma((pairs, 3)),
+            dma((pairs, vpair_count)),
+            dma((zs, 2)),
+            dma((zs, 2)),
+            dma((zs, 2)),
         ],
         compiler_params=pltpu.CompilerParams(
             collective_id=1, has_side_effects=True, vmem_limit_bytes=60 * 1024 * 1024
         ),
         cost_estimate=pl.CostEstimate(flops=10**10, bytes_accessed=10**7, transcendentals=0),
-    )(factors_pad, amps_pad)
-
-
-def ladder_middle(factors_pad, cols_pad, half_done, kernel_sub, rank_count):
+    )(factors_pad, amps_pad, kernel)
+
+
+def ladder_middle(cols_pad, line, half, kernel_sub, rank_count):
     count, block, depth = cols_pad.shape
-    pairs = half_done.shape[0]
+    pairs = half.shape[0]
     cols = kernel_sub.shape[1]
     rows = count * block
     points = kernel_sub.shape[0]
@@ -445,12 +539,10 @@
             pltpu.VMEM((4, cols, depth), jnp.bfloat16),
             pltpu.VMEM((pairs * cols, rows), jnp.float32),
             dma((1,)),
-            dma((pairs, 3)),
-            dma((pairs, count)),
+            dma((pairs,)),
             dma((rank_count, count)),
             dma((rank_count,)),
-            dma((zs,)),
-            dma((zs, 3)),
+            dma((zs, 2)),
             dma((zs,)),
             dma((pairs, 3)),
             dma((pairs, count)),
@@ -461,7 +553,7 @@
         cost_estimate=pl.CostEstimate(
             flops=4 * pairs * points * rows * cols, bytes_accessed=4 * points * rows, transcendentals=0
         ),
-    )(factors_pad, cols_pad, half_done, kernel_sub)
+    )(cols_pad, line, half, kernel_sub)
 
 
 CUTS = 4
@@ -600,7 +692,8 @@
     def _(p):
         other_copy(p).start()
 
-    turned[...] = cols_ref[...].T
+    flat = jnp.concatenate([cols_ref[j, :rows, :] for j in range(count)], axis=0)
+    turned[...] = flat.T
     stages = ((1, give), (3, meet), (5, close), (7, land), (8, settle))
     last = stages[-1][0]
 
@@ -644,10 +737,10 @@
                 res_copy(2 * t + e, h).wait()
 
 
-def ladder_tail(back, cols_flat, other_turned, row_energy, virt_energy):
+def ladder_tail(back, cols_pad, other_turned, row_energy, virt_energy):
     pairs, count, block, cols = back.shape
     rows = other_turned.shape[0]
-    virt_count, depth = cols_flat.shape
+    virt_count, depth = virt_energy.shape[1], cols_pad.shape[2]
     turns = pairs // 2
     hbm = pl.BlockSpec(memory_space=pl.ANY)
     vmem = pl.BlockSpec(memory_space=pltpu.VMEM)
@@ -693,7 +786,7 @@
             flops=2 * pairs * rows * virt_count * depth, bytes_accessed=8 * pairs * rows * virt_count,
             transcendentals=0,
         ),
-    )(back, cols_flat, other_turned, row_energy, virt_energy)
+    )(back, cols_pad, other_turned, row_energy, virt_energy)
 
 
 def fast_shards(amplitudes, factors, kernel, other_terms, virt_energy, pair_energy):
@@ -701,34 +794,24 @@
     rank_count = lax.axis_size("rank")
     pair_count, row_block, _ = amplitudes.shape
     virt_count = row_block * vpair_count
-    right_block = kernel.shape[1]
     block = -(-row_block // 16) * 16
+    tall = -(-row_block // 64) * 64
     col_block = amplitudes.shape[2]
     deep = -(-col_block // 16) * 16
-    kernel_sub = lax.all_to_all(kernel, "vpair", split_axis=1, concat_axis=0, tiled=True)
     factors_pad = jnp.pad(factors, ((0, block - row_block), (0, 0)))
     amps_pad = jnp.pad(
-        amplitudes.transpose(2, 0, 1), ((0, deep - col_block), (0, 0), (0, block - row_block))
-    ).reshape(deep, pair_count * block)
-    cols_pad, amps = front_gather(factors_pad, amps_pad, vpair_count, rank_count)
-    factor_cols = cols_pad[:, :row_block].reshape(virt_count, right_block)
-    cols_deep = jnp.pad(
-        factor_cols.reshape(rank_count, col_block, right_block), ((0, 0), (0, deep - col_block), (0, 0))
-    ).reshape(rank_count * deep, right_block)
-    half_done = jnp.einsum(
-        "sm,sh->mh",
-        amps.reshape(rank_count * deep, pair_count * block),
-        cols_deep,
-        preferred_element_type=jnp.float32,
-    ).astype(jnp.bfloat16)
-    half_done = half_done.reshape(pair_count, block, right_block)
-    back = ladder_middle(factors_pad, cols_pad, half_done, kernel_sub, rank_count)
+        amplitudes.transpose(2, 0, 1), ((0, deep - col_block), (0, 0), (0, tall - row_block))
+    ).reshape(deep, pair_count * tall)
+    cols_pad, half, kernel_sub, line = front_gather(
+        factors_pad, amps_pad, kernel, pair_count, col_block, vpair_count, rank_count
+    )
+    back = ladder_middle(cols_pad, line, half, kernel_sub, rank_count)
     row_energy = lax.dynamic_slice_in_dim(
         virt_energy, lax.axis_index("vpair") * row_block, row_block, 0
     )
     shifted = row_energy[None, :, None] - pair_energy[:, None, None]
     residual, squares = ladder_tail(
-        back, factor_cols, other_terms.transpose(1, 0, 2), shifted, virt_energy[None, :]
+        back, cols_pad, other_terms.transpose(1, 0, 2), shifted, virt_energy[None, :]
     )
     update_rms = jnp.sqrt(squares[0, 0] / (pair_count * virt_count * virt_count) + epsilon)
     return (residual.transpose(1, 0, 2), update_rms)
@@ -741,6 +824,7 @@
         vpair_count == 4
         and rank_count == 8
         and amplitudes.shape[0] == 8
+        and amplitudes.shape[1] == 2 * amplitudes.shape[2]
         and kernel.shape[1] % (128 * vpair_count) == 0
     )
     body = fast_shards if fits else shards

time: 425 us -> 391 us (0.920)
  matrix products: 11.5 us -> 0 us
  Pallas kernels: 380 us -> 370 us
  local copies, waits for them, and re-layouts: 23.8 us -> 16.8 us
  starting transfers between devices: 5.32 us -> 0 us
    pallas_call x1, Pallas kernels: 206 us -> 127 us  [ladder_middle(): pl.pallas_call(functools.partial(middle_kernel, zs), out_shape=jax.ShapeD...]
    pallas_call x1, Pallas kernels: 73.9 us -> 143 us  [front_gather(): pl.pallas_call(functools.partial(front_kernel, zs, col_block), out_shape=...]
    dot_general x1 -> x0, matrix products: 11.5 us -> none  [fast_shards(): jnp.einsum('sm,sh->mh', amps.reshape(rank_count * deep, pair_count * bloc...]
    all_to_all x1 -> x0, starting transfers between devices: 5.32 us -> none  [fast_shards(): lax.all_to_all(kernel, 'vpair', split_axis=1, concat_axis=0, tiled=True)]
    all_to_all x1 -> x0, local copies, waits for them, and re-layouts: 4.53 us -> none  [fast_shards(): lax.all_to_all(kernel, 'vpair', split_axis=1, concat_axis=0, tiled=True)]
    another operation x1 -> x0, local copies, waits for them, and re-layouts: 4.29 us -> none  [fast_shards(): factor_cols.reshape(rank_count, col_block, right_block)]
    unnamed x11 -> x3, local copies, waits for them, and re-layouts: 9.99 us -> 9.97 us
  transfers between devices with their start and end apart: 1 -> 0, of which waited for: 0 -> 0; matrix products, arithmetic and copies ran while one was open for 5% -> 0% of each run, Pallas kernels for 17% -> 0%
where the time goes in v3:
time: 391 us; the launch traced here: 390 us
  Pallas kernels  370 us (95%)
  local copies, waits for them, and re-layouts  16.8 us (4%)
    pallas_call x1, Pallas kernels, front_gather(): pl.pallas_call(functools.partial(front_kernel, zs, col_block), out_shape=...  143 us
    pallas_call x1, Pallas kernels, ladder_middle(): pl.pallas_call(functools.partial(middle_kernel, zs), out_shape=jax.ShapeD...  127 us
    pallas_call x1, Pallas kernels, ladder_tail(): pl.pallas_call(tail_kernel, out_shape=(jax.ShapeDtypeStruct((rows, pairs,...  100 us
    unnamed x3, local copies, waits for them, and re-layouts  9.97 us

profile of v3, /device:TPU:0, one launch (start us, length us, event | category | flops | bytes accessed | tf_op | source)
XLA Modules:
  0.0 390.5 jit_solution(9042804454871724628)
XLA Ops:
  0.6 0.0 copy-start
  0.6 0.8 dynamic_slice.3
  1.4 1.3 broadcast_in_dim.2.virt_ref
  2.7 2.0 pad.8.own_ref
  4.7 1.3 pad.9
  5.9 1.6 reshape.60.amp_ref
  7.5 0.0 copy-done
  7.5 1.2 broadcast_subtract_fusion.rowen_ref
  8.7 142.5 %shard_map.77 = (bf16[4,304,1024]{2,1,0:T(8,128)(2,1)}, bf16[8,4,304,256]{3,2,1,0:T(8,128)(2,1)}, bf16[8192,256]{1,0:T(8,128)(2,1)}, bf16[4,2,304,1024]{3,2,1,0:T(8,128)(2,1)}) custom-call(bf16[304,1024]{1,0:T(8,128)(2,1)} %pad.8.own_ref, bf16[160,2560]{1,0:T(8,128)(2,1)} %reshape.60.amp_ref, bf16[2048,1024]{1,0:T(8,128)(2,1)} %kern_ref.1), custom_call_target="tpu_custom_call" | custom-call | flops 10000000000 | bytes 10000000 | tf_op jit(solution)/shard_map/pallas_call | solution.py:482
  151.2 127.3 %shard_map.78.back_ref = bf16[8,4,304,256]{3,2,1,0:T(8,128)(2,1)} custom-call(bf16[4,304,1024]{2,1,0:T(8,128)(2,1)} %get-tuple-element.8.cols_ref, bf16[4,2,304,1024]{3,2,1,0:T(8,128)(2,1)} %get-tuple-element.9.line_ref, bf16[8,4,304,256]{3,2,1,0:T(8,128)(2,1)} %get-tuple-element.10.half_ref, bf16[8192,256]{1,0:T(8,128)(2,1)} %get-tuple-element.11.kern_ref), custom_call_target="tpu_custom_call" | custom-call | flops 81604378624 | bytes 39845888 | tf_op jit(solution)/shard_map/pallas_call | solution.py:530
  278.5 100.1 %shard_map.79 = (f32[300,8,1200]{2,1,0:T(8,128)}, f32[1,1]{1,0:T(1,128)}) custom-call(bf16[8,4,304,256]{3,2,1,0:T(8,128)(2,1)} %shard_map.78.back_ref, bf16[4,304,1024]{2,1,0:T(8,128)(2,1)} %get-tuple-element.8.cols_ref, f32[300,8,1200]{2,1,0:T(8,128)} %bitcast.6, f32[8,300,1]{2,1,0:T(8,128)} %broadcast_subtract_fusion.rowen_ref, ...), custom_call_target="tpu_custom_call" | custom-call | flops 5898240000 | bytes 23040000 | tf_op jit(solution)/shard_map/pallas_call | solution.py:750
  379.4 10.0 %copy.9 = f32[8,300,1200]{2,0,1:T(8,128)} copy(f32[8,300,1200]{2,0,1:T(8,128)} %bitcast.4) | data formatting | bytes 23040000
Async XLA Ops:
  0.6 6.9 %copy-start = (f32[8]{0:T(128)S(1)}, f32[8]{0:T(128)}, u32[]{:S(2)}) copy-start(f32[8]{0:T(128)} %param.11) | copy-start | bytes 100

commit v4 on v3

--- a/solution.py
+++ b/solution.py
@@ -65,8 +65,8 @@
 
 
 def middle_kernel(
-    zs, cols_ref, line_ref, half_ref, kern_ref, out_ref, fall, hrecv, hturn, kturn, acc,
-    loc_sem, hr, fr, mr, xsend, msend, bs, br,
+    zs, cols_ref, line_ref, half_ref, kern_ref, early_ref, out_ref, fall, hrecv, hturn, kturn, late, acc,
+    loc_sem, hr, fr, mr, xsend, msend, bs, br, far_sem, ks, kr,
 ):
     v = lax.axis_index("vpair")
     r = lax.axis_index("rank")
@@ -81,12 +81,14 @@
     group = 2
     groups = pairs // group
     tall = group * cols
-
-    def rank_at(k, side):
-        return ((z + k) % zs) * 2 + side
+    in_middle = jnp.logical_or(z == 1, z == 2)
+
+    def line_at(k):
+        return jnp.where(z < 2, (z + k) % zs, (z + zs - k) % zs)
 
     barrier = pltpu.get_barrier_semaphore()
-    peers = [(at, r) for at in near] + [(v, mate)]
+    line_peers = [(v, ((z + k) % zs) * 2 + core) for k in (1, zs - 1)]
+    peers = [(at, r) for at in near] + [(v, mate)] + line_peers
     for peer in peers:
         pl.semaphore_signal(barrier, inc=1, device_id=peer, device_id_type=MESH_IDS)
     pl.semaphore_wait(barrier, len(peers))
@@ -102,48 +104,77 @@
 
     def line_copy(k, slot):
         at = vd if slot else v
-        rr = rank_at(k, core)
+        rr = line_at(k) * 2 + core
         return pltpu.make_async_copy(line_ref.at[rr // 2, slot], fall.at[rr, at], fr.at[rr, at])
 
+    def far_copy(slot):
+        at = vd if slot else v
+        far, to = jnp.where(z == 1, zs - 1, 0), jnp.where(z == 1, 0, zs - 1)
+        rr = far * 2 + core
+        return remote(
+            line_ref.at[far, slot], fall.at[rr, at], far_sem.at[slot], fr.at[rr, at], (v, to * 2 + core)
+        )
+
     def side_copy(k, j):
-        rr = rank_at(k, core)
-        return remote(line_ref.at[rr // 2, 0], fall.at[rr, v], xsend.at[k, j], fr.at[rr, v], (near[j], r))
+        rr = line_at(k) * 2 + core
+        src = line_ref.at[rr // 2, 0] if k < zs - 1 else fall.at[rr, v]
+        return remote(src, fall.at[rr, v], xsend.at[k, j], fr.at[rr, v], (near[j], r))
 
     def mate_copy(k):
-        rr = rank_at(k, core)
+        rr = line_at(k) * 2 + core
         return remote(fall.at[rr], fall.at[rr], msend.at[k], mr.at[rr], (v, mate))
 
     def shard_wait(rr, at):
         pltpu.make_async_copy(fall.at[rr, at], fall.at[rr, at], fr.at[rr, at]).wait()
 
-    def block_wait(rr):
-        pltpu.make_async_copy(fall.at[rr], fall.at[rr], mr.at[rr]).wait()
+    def late_part(at):
+        side = pl.ds(pl.multiple_of((1 - core) * depth, depth), depth)
+        return kern_ref.at[side, pl.ds(pl.multiple_of(at * cols, cols), cols)]
+
+    def late_copy(j):
+        return remote(late_part(near[j]), late.at[v], ks.at[j], kr.at[v], (near[j], r))
 
     def finish(k):
-        rr = rank_at(k, core)
-        for at in (v, vx, vy, vd):
+        rr = line_at(k) * 2 + core
+        for at in (v, vx, vy, vd)[k == zs - 1 :]:
             shard_wait(rr, at)
         mate_copy(k).start()
 
+    def spread_last():
+        shard_wait(line_at(zs - 1) * 2 + core, v)
+        for j in (0, 1):
+            side_copy(zs - 1, j).start()
+        for j in (0, 1, 2):
+            late_copy(j).start()
+
     own_block = pltpu.make_async_copy(cols_ref, fall.at[r], loc_sem.at[0])
     mate_block = remote(cols_ref, fall.at[r], msend.at[0], mr.at[r], (v, mate))
+    own_late = pltpu.make_async_copy(late_part(v), late.at[v], kr.at[v])
     own_block.start()
-    mate_block.start()
-    for k in range(1, zs):
+    for k in range(1, zs - 1):
         for j in (0, 1):
             side_copy(k, j).start()
+
+    @pl.when(in_middle)
+    def _():
+        for slot in (0, 1):
+            far_copy(slot).start()
 
     @pl.loop(0, pairs)
     def _(i):
         own_half(i).start()
 
-    for k in range(1, zs):
+    for k in range(1, zs - 1):
         for slot in (0, 1):
             line_copy(k, slot).start()
 
-    def turn_kernel(rr, slot):
-        start = pl.multiple_of(rr * depth, depth)
-        kturn[slot] = kern_ref[pl.ds(start, depth), :].T
+    @pl.when(in_middle)
+    def _():
+        for slot in (0, 1):
+            line_copy(zs - 1, slot).start()
+
+    mate_block.start()
+    own_late.start()
 
     def compute(rr, slot, g):
         at = pl.multiple_of(g * tall, tall)
@@ -156,10 +187,8 @@
             preferred_element_type=jnp.float32,
         )
 
-    turn_kernel(r, 0)
-    turn_kernel(mate, 1)
+    kturn[0] = early_ref[z].T
     own_block.wait()
-    block_wait(mate)
 
     @pl.loop(0, groups)
     def _(g):
@@ -169,39 +198,23 @@
             own_half(i).wait()
             hturn[pl.ds(at + e * cols, cols), :] = hrecv[i].reshape(rows, cols).T
         acc[pl.ds(at, tall), :] = compute(r, 0, g)
-        acc[pl.ds(at, tall), :] += compute(mate, 1, g)
-
-        @pl.when(g == 2)
-        def _():
-            finish(1)
-
-    @pl.loop(0, 2)
-    def _(odd):
-        rr = rank_at(1, core + odd - 2 * odd * core)
-
-        @pl.when(odd == 1)
-        def _():
-            block_wait(rr)
-
-        turn_kernel(rr, 0)
+
+    @pl.loop(1, zs)
+    def _(k):
+        for n in range(1, zs):
+
+            @pl.when(k == n)
+            def _():
+                finish(n)
+                if n == zs - 2:
+                    spread_last()
+
+        kturn[k] = early_ref[line_at(k)].T
 
         @pl.loop(0, groups)
         def _(g):
-            @pl.when(jnp.logical_and(odd == 0, g == 2))
-            def _():
-                finish(2)
-
-            @pl.when(jnp.logical_and(odd == 1, g == 2))
-            def _():
-                finish(3)
-
             at = pl.multiple_of(g * tall, tall)
-            acc[pl.ds(at, tall), :] += compute(rr, 0, g)
-
-    @pl.loop(0, 4)
-    def _(n):
-        side = n % 2
-        turn_kernel(rank_at(n // 2 + 2, core + side - 2 * side * core), n)
+            acc[pl.ds(at, tall), :] += compute(line_at(k) * 2 + core, k, g)
 
     def back_copy(i, j):
         return remote(hrecv.at[i, near[j]], out_ref.at[i, v], bs.at[i, j], br.at[i, v], (near[j], r))
@@ -209,38 +222,44 @@
     def own_back(i):
         return pltpu.make_async_copy(hrecv.at[i, v], out_ref.at[i, v], br.at[i, v])
 
-    @pl.loop(0, 2 * groups)
-    def _(m):
-        g = m // 2
-        k = m % 2 + 2
-
+    @pl.loop(0, groups)
+    def _(g):
         at = pl.multiple_of(g * tall, tall)
 
-        @pl.loop(0, 2)
-        def _(side):
-            rr = rank_at(k, core + side - 2 * side * core)
-
-            @pl.when(jnp.logical_and(g == 0, side == 1))
+        @pl.loop(0, count)
+        def _(j):
+            where = jnp.where(j < 2, jnp.where(j == 0, v, vx), jnp.where(j == 2, vy, vd))
+            rr = where * 2 + 1 - core
+
+            @pl.when(g == 0)
             def _():
-                block_wait(rr)
-
-            acc[pl.ds(at, tall), :] += compute(rr, (k - 2) * 2 + side, g)
-
-        @pl.when(k == 3)
-        def _():
-            for e in range(group):
-                i = g * group + e
-                piece = acc[pl.ds(at + e * cols, cols), :].astype(jnp.bfloat16)
-                hrecv[i] = piece.T.reshape(count, block, cols)
-                for j in (0, 1, 2):
-                    back_copy(i, j).start()
-                own_back(i).start()
+                pltpu.make_async_copy(fall.at[rr], fall.at[rr], mr.at[rr]).wait()
+                pltpu.make_async_copy(late.at[where], late.at[where], kr.at[where]).wait()
+                kturn[j] = late[where].T
+
+            acc[pl.ds(at, tall), :] += compute(rr, j, g)
+
+        for e in range(group):
+            i = g * group + e
+            piece = acc[pl.ds(at + e * cols, cols), :].astype(jnp.bfloat16)
+            hrecv[i] = piece.T.reshape(count, block, cols)
+            for j in (0, 1, 2):
+                back_copy(i, j).start()
+            own_back(i).start()
 
     mate_block.wait_send()
     for k in range(1, zs):
         for j in (0, 1):
             side_copy(k, j).wait_send()
         mate_copy(k).wait_send()
+
+    @pl.when(in_middle)
+    def _():
+        for slot in (0, 1):
+            far_copy(slot).wait_send()
+
+    for j in (0, 1, 2):
+        late_copy(j).wait_send()
 
     @pl.loop(0, pairs)
     def _(i):
@@ -251,8 +270,8 @@
 
 
 def front_kernel(
-    zs, col_block, own_ref, amp_ref, kern_ref, cols_ref, half_ref, z_ref, line_ref,
-    cbuf, amps, zbuf, deep, hstage,
+    zs, col_block, own_ref, amp_ref, kern_ref, cols_ref, half_ref, z_ref, line_ref, turn_ref,
+    cbuf, amps, zbuf, deep, hstage, tbuf,
     mine, cs, cr, us, ds, ms, ar, ks, kr, hs, hr, lu, ld, lr,
 ):
     v = lax.axis_index("vpair")
@@ -265,7 +284,7 @@
     has_up, has_down = z + 1 < zs, z >= 1
     up_to, down_to = ((z + 1) % zs) * 2 + core, ((z + zs - 1) % zs) * 2 + core
     pairs, count, block, cols = half_ref.shape
-    points = kern_ref.shape[0]
+    depth = own_ref.shape[1]
     rank_count, deep_block = amps.shape[:2]
     groups = hstage.shape[0]
     wide = hstage.shape[1]
@@ -293,13 +312,11 @@
         return remote(own_ref, cbuf.at[v], cs.at[j], cr.at[v], (near[j], r))
 
     def part_of(at):
-        return kern_ref.at[:, pl.ds(pl.multiple_of(at * cols, cols), cols)]
-
-    def rows_of(at):
-        return z_ref.at[pl.ds(pl.multiple_of(at * points, points), points), :]
+        side = pl.ds(pl.multiple_of(core * depth, depth), depth)
+        return kern_ref.at[side, pl.ds(pl.multiple_of(at * cols, cols), cols)]
 
     def kern_copy(j):
-        return remote(part_of(near[j]), rows_of(v), ks.at[j], kr.at[v], (near[j], r))
+        return remote(part_of(near[j]), z_ref.at[v], ks.at[j], kr.at[v], (near[j], r))
 
     def line_copy(src, at, slot, sem, to):
         return remote(src, line_ref.at[at, slot], sem.at[at, slot], lr.at[at, slot], (v, to))
@@ -330,7 +347,7 @@
     own_cols = pltpu.make_async_copy(own_ref, cbuf.at[v], mine.at[0])
     own_amps = pltpu.make_async_copy(amp_ref, amps.at[r], mine.at[1])
     own_in = pltpu.make_async_copy(part_of(v), zbuf, mine.at[2])
-    own_out = pltpu.make_async_copy(zbuf, rows_of(v), mine.at[2])
+    own_out = pltpu.make_async_copy(zbuf, z_ref.at[v], mine.at[2])
     own_cols.start()
     own_amps.start()
     own_in.start()
@@ -369,18 +386,22 @@
             for slot in (0, 1):
                 arrive(line_ref.at[low, slot], lr.at[low, slot])
 
-                @pl.when(has_up)
-                def _():
-                    line_copy(line_ref.at[low, slot], low, slot, lu, up_to).start()
+                if s < zs - 2:
+
+                    @pl.when(has_up)
+                    def _():
+                        line_copy(line_ref.at[low, slot], low, slot, lu, up_to).start()
 
         @pl.when(z + s < zs)
         def _():
             for slot in (0, 1):
                 arrive(line_ref.at[high, slot], lr.at[high, slot])
 
-                @pl.when(has_down)
-                def _():
-                    line_copy(line_ref.at[high, slot], high, slot, ld, down_to).start()
+                if s < zs - 2:
+
+                    @pl.when(has_down)
+                    def _():
+                        line_copy(line_ref.at[high, slot], high, slot, ld, down_to).start()
 
     for s in range(1, zs - 1):
         amps_step(s)
@@ -423,10 +444,14 @@
                 half_copy(i, j).start()
             own_half(i).start()
 
-    for s in range(1, zs):
+    flat = jnp.concatenate([cbuf[j, : per * col_block, :] for j in range(count)], axis=0)
+    tbuf[...] = flat.T
+    turn_out = pltpu.make_async_copy(tbuf, turn_ref, mine.at[1])
+    turn_out.start()
+    for s in range(1, zs - 1):
         line_step(s)
     for at in near:
-        arrive(rows_of(at), kr.at[at])
+        arrive(z_ref.at[at], kr.at[at])
 
     @pl.loop(0, pairs)
     def _(i):
@@ -437,6 +462,7 @@
 
     own_out.wait()
     cols_out.wait()
+    turn_out.wait()
     for j in (0, 1, 2):
         cols_copy(j).wait_send()
         kern_copy(j).wait_send()
@@ -450,12 +476,14 @@
         @pl.when(jnp.logical_and(z >= s, has_up))
         def _():
             amps_copy(amp_ref, r, us.at[s], up_to).wait_send()
-            line_sent((z + zs - s) % zs, lu, up_to)
+            if s < zs - 2:
+                line_sent((z + zs - s) % zs, lu, up_to)
 
         @pl.when(jnp.logical_and(z + s < zs, has_down))
         def _():
             amps_copy(amp_ref, r, ds.at[s], down_to).wait_send()
-            line_sent((z + s) % zs, ld, down_to)
+            if s < zs - 2:
+                line_sent((z + s) % zs, ld, down_to)
 
         if s:
 
@@ -471,7 +499,6 @@
 def front_gather(factors_pad, amps_pad, kernel, pairs, col_block, vpair_count, rank_count):
     zs = rank_count // 2
     block, right_block = factors_pad.shape
-    points = kernel.shape[0]
     cols = right_block // vpair_count
     deep_block, width = amps_pad.shape
     groups = pairs // 2
@@ -484,17 +511,19 @@
         out_shape=(
             like(vpair_count, block, right_block),
             like(pairs, vpair_count, block, cols),
-            like(points * vpair_count, cols),
+            like(vpair_count, right_block, cols),
             like(zs, 2, block, right_block),
+            like(right_block, rank_count * col_block),
         ),
         in_specs=[hbm, hbm, hbm],
-        out_specs=(hbm, hbm, hbm, hbm),
+        out_specs=(hbm, hbm, hbm, hbm, hbm),
         scratch_shapes=[
             bf16(vpair_count, block, right_block),
             bf16(rank_count, deep_block, width),
-            bf16(points, cols),
+            bf16(right_block, cols),
             bf16(rank_count * deep_block, right_block),
             bf16(groups, width // groups, right_block),
+            bf16(right_block, rank_count * col_block),
             dma((3,)),
             dma((3,)),
             dma((vpair_count,)),
@@ -517,12 +546,12 @@
     )(factors_pad, amps_pad, kernel)
 
 
-def ladder_middle(cols_pad, line, half, kernel_sub, rank_count):
+def ladder_middle(cols_pad, line, half, kernel, early, rank_count):
     count, block, depth = cols_pad.shape
     pairs = half.shape[0]
-    cols = kernel_sub.shape[1]
+    cols = early.shape[2]
     rows = count * block
-    points = kernel_sub.shape[0]
+    points = rank_count * depth
     zs = rank_count // 2
     hbm = pl.BlockSpec(memory_space=pl.ANY)
     vmem = pl.BlockSpec(memory_space=pltpu.VMEM)
@@ -530,13 +559,14 @@
     return pl.pallas_call(
         functools.partial(middle_kernel, zs),
         out_shape=jax.ShapeDtypeStruct((pairs, count, block, cols), jnp.bfloat16),
-        in_specs=[hbm, hbm, hbm, vmem],
+        in_specs=[hbm, hbm, hbm, hbm, vmem],
         out_specs=hbm,
         scratch_shapes=[
             pltpu.VMEM((rank_count, count, block, depth), jnp.bfloat16),
             pltpu.VMEM((pairs, count, block, cols), jnp.bfloat16),
             pltpu.VMEM((pairs * cols, rows), jnp.bfloat16),
             pltpu.VMEM((4, cols, depth), jnp.bfloat16),
+            pltpu.VMEM((count, depth, cols), jnp.bfloat16),
             pltpu.VMEM((pairs * cols, rows), jnp.float32),
             dma((1,)),
             dma((pairs,)),
@@ -546,6 +576,9 @@
             dma((zs,)),
             dma((pairs, 3)),
             dma((pairs, count)),
+            dma((2,)),
+            dma((3,)),
+            dma((count,)),
         ],
         compiler_params=pltpu.CompilerParams(
             collective_id=0, has_side_effects=True, vmem_limit_bytes=62 * 1024 * 1024
@@ -553,15 +586,15 @@
         cost_estimate=pl.CostEstimate(
             flops=4 * pairs * points * rows * cols, bytes_accessed=4 * points * rows, transcendentals=0
         ),
-    )(cols_pad, line, half, kernel_sub)
+    )(cols_pad, line, half, kernel, early)
 
 
 CUTS = 4
 
 
 def tail_kernel(
-    back_ref, cols_ref, other_ref, rowen_ref, virt_ref, res_ref, sq_ref,
-    turned, part, msend, mrecv, zsend, outer, inner, fin, oth, sq, sqall,
+    back_ref, turned, other_ref, rowen_ref, virt_ref, res_ref, sq_ref,
+    part, msend, mrecv, zsend, outer, inner, fin, oth, sq, sqall,
     ms, mr, zs_sem, outr, inr, fs, fr, osem, rsem, qs, qr,
 ):
     v = lax.axis_index("vpair")
@@ -692,8 +725,6 @@
     def _(p):
         other_copy(p).start()
 
-    flat = jnp.concatenate([cols_ref[j, :rows, :] for j in range(count)], axis=0)
-    turned[...] = flat.T
     stages = ((1, give), (3, meet), (5, close), (7, land), (8, settle))
     last = stages[-1][0]
 
@@ -737,10 +768,10 @@
                 res_copy(2 * t + e, h).wait()
 
 
-def ladder_tail(back, cols_pad, other_turned, row_energy, virt_energy):
+def ladder_tail(back, turned, other_turned, row_energy, virt_energy):
     pairs, count, block, cols = back.shape
     rows = other_turned.shape[0]
-    virt_count, depth = virt_energy.shape[1], cols_pad.shape[2]
+    depth, virt_count = turned.shape
     turns = pairs // 2
     hbm = pl.BlockSpec(memory_space=pl.ANY)
     vmem = pl.BlockSpec(memory_space=pltpu.VMEM)
@@ -756,7 +787,6 @@
         in_specs=[vmem, vmem, hbm, vmem, vmem],
         out_specs=(hbm, vmem),
         scratch_shapes=[
-            bf16(depth, virt_count),
             f32(turns, rows, virt_count),
             bf16(turns, rows, virt_count),
             bf16(turns, rows, virt_count),
@@ -786,7 +816,7 @@
             flops=2 * pairs * rows * virt_count * depth, bytes_accessed=8 * pairs * rows * virt_count,
             transcendentals=0,
         ),
-    )(back, cols_pad, other_turned, row_energy, virt_energy)
+    )(back, turned, other_turned, row_energy, virt_energy)
 
 
 def fast_shards(amplitudes, factors, kernel, other_terms, virt_energy, pair_energy):
@@ -802,16 +832,16 @@
     amps_pad = jnp.pad(
         amplitudes.transpose(2, 0, 1), ((0, deep - col_block), (0, 0), (0, tall - row_block))
     ).reshape(deep, pair_count * tall)
-    cols_pad, half, kernel_sub, line = front_gather(
+    cols_pad, half, early, line, turned = front_gather(
         factors_pad, amps_pad, kernel, pair_count, col_block, vpair_count, rank_count
     )
-    back = ladder_middle(cols_pad, line, half, kernel_sub, rank_count)
+    back = ladder_middle(cols_pad, line, half, kernel, early, rank_count)
     row_energy = lax.dynamic_slice_in_dim(
         virt_energy, lax.axis_index("vpair") * row_block, row_block, 0
     )
     shifted = row_energy[None, :, None] - pair_energy[:, None, None]
     residual, squares = ladder_tail(
-        back, cols_pad, other_terms.transpose(1, 0, 2), shifted, virt_energy[None, :]
+        back, turned, other_terms.transpose(1, 0, 2), shifted, virt_energy[None, :]
     )
     update_rms = jnp.sqrt(squares[0, 0] / (pair_count * virt_count * virt_count) + epsilon)
     return (residual.transpose(1, 0, 2), update_rms)

time: 391 us -> 373 us (0.954)
  Pallas kernels: 370 us -> 353 us
    pallas_call x1, Pallas kernels: 143 us -> 121 us  [front_gather(): pl.pallas_call(functools.partial(front_kernel, zs, col_block), out_shape=...]
    pallas_call x1, Pallas kernels: 127 us -> 132 us  [ladder_middle(): pl.pallas_call(functools.partial(middle_kernel, zs), out_shape=jax.ShapeD...]
where the time goes in v4:
time: 373 us
  Pallas kernels  353 us (95%)
  local copies, waits for them, and re-layouts  16.8 us (5%)
    pallas_call x1, Pallas kernels, ladder_middle(): pl.pallas_call(functools.partial(middle_kernel, zs), out_shape=jax.ShapeD...  132 us
    pallas_call x1, Pallas kernels, front_gather(): pl.pallas_call(functools.partial(front_kernel, zs, col_block), out_shape=...  121 us
    pallas_call x1, Pallas kernels, ladder_tail(): pl.pallas_call(tail_kernel, out_shape=(jax.ShapeDtypeStruct((rows, pairs,...  99.7 us
    unnamed x3, local copies, waits for them, and re-layouts  9.97 us

profile of v4, /device:TPU:0, one launch (start us, length us, event | category | flops | bytes accessed | tf_op | source)
XLA Modules:
  0.0 373.0 jit_solution(10772064006077337201)
XLA Ops:
  0.6 0.0 copy-start
  0.6 0.8 dynamic_slice.3
  1.4 1.3 broadcast_in_dim.2.virt_ref
  2.7 2.0 pad.8.own_ref
  4.7 1.3 pad.9
  6.0 1.6 reshape.60.amp_ref
  7.5 0.0 copy-done
  7.5 1.2 broadcast_subtract_fusion.rowen_ref
  8.7 121.1 %shard_map.77 = (bf16[4,304,1024]{2,1,0:T(8,128)(2,1)}, bf16[8,4,304,256]{3,2,1,0:T(8,128)(2,1)}, bf16[4,1024,256]{2,1,0:T(8,128)(2,1)}, bf16[4,2,304,1024]{3,2,1,0:T(8,128)(2,1)}, bf16[1024,1200]{1,0:T(8,128)(2,1)}) custom-call(bf16[304,1024]{1,0:T(8,128)(2,1)} %pad.8.own_ref, bf16[160,2560]{1,0:T(8,128)(2,1)} %reshape.60.amp_ref, bf16[2048,1024]{1,0:T(8,128)(2,1)} %kern_ref.3), custom_call_target="tpu_custom_call" | custom-call | flops 10000000000 | bytes 10000000 | tf_op jit(solution)/shard_map/pallas_call | solution.py:509
  129.8 131.8 %shard_map.78.back_ref = bf16[8,4,304,256]{3,2,1,0:T(8,128)(2,1)} custom-call(bf16[4,304,1024]{2,1,0:T(8,128)(2,1)} %get-tuple-element.9.cols_ref, bf16[4,2,304,1024]{3,2,1,0:T(8,128)(2,1)} %get-tuple-element.10.line_ref, bf16[8,4,304,256]{3,2,1,0:T(8,128)(2,1)} %get-tuple-element.11.half_ref, bf16[2048,1024]{1,0:T(8,128)(2,1)} %kern_ref.3, ...), custom_call_target="tpu_custom_call" | custom-call | flops 81604378624 | bytes 39845888 | tf_op jit(solution)/shard_map/pallas_call | solution.py:559
  261.6 99.7 %shard_map.79 = (f32[300,8,1200]{2,1,0:T(8,128)}, f32[1,1]{1,0:T(1,128)}) custom-call(bf16[8,4,304,256]{3,2,1,0:T(8,128)(2,1)} %shard_map.78.back_ref, bf16[1024,1200]{1,0:T(8,128)(2,1)} %get-tuple-element.13.turned, f32[300,8,1200]{2,1,0:T(8,128)} %bitcast.6, f32[8,300,1]{2,1,0:T(8,128)} %broadcast_subtract_fusion.rowen_ref, f32[1,1200]{1,0:T(1,128)} %broadcast_in_dim.2.virt_ref), custom_call_target="tpu_custom_call" | custom-call | flops 5898240000 | bytes 23040000 | tf_op jit(solution)/shard_map/pallas_call | solution.py:781
  361.9 10.0 %copy.9 = f32[8,300,1200]{2,0,1:T(8,128)} copy(f32[8,300,1200]{2,0,1:T(8,128)} %bitcast.4) | data formatting | bytes 23040000
Async XLA Ops:
  0.6 6.9 %copy-start = (f32[8]{0:T(128)S(1)}, f32[8]{0:T(128)}, u32[]{:S(2)}) copy-start(f32[8]{0:T(128)} %param.11) | copy-start | bytes 100

commit v5 on v4

--- a/solution.py
+++ b/solution.py
@@ -589,7 +589,7 @@
     )(cols_pad, line, half, kernel, early)
 
 
-CUTS = 4
+CUTS = 7
 
 
 def tail_kernel(
@@ -725,7 +725,7 @@
     def _(p):
         other_copy(p).start()
 
-    stages = ((1, give), (3, meet), (5, close), (7, land), (8, settle))
+    stages = ((1, give), (3, meet), (5, close), (7, land), (9, settle))
     last = stages[-1][0]
 
     @pl.loop(0, turns + -(-last // CUTS))

time: 373 us -> 369 us (0.989)
  Pallas kernels: 353 us -> 348 us
    pallas_call x1, Pallas kernels: 99.7 us -> 95.3 us  [ladder_tail(): pl.pallas_call(tail_kernel, out_shape=(jax.ShapeDtypeStruct((rows, pairs,...]
where the time goes in v5:
time: 369 us
  Pallas kernels  348 us (94%)
  local copies, waits for them, and re-layouts  16.8 us (5%)
    pallas_call x1, Pallas kernels, ladder_middle(): pl.pallas_call(functools.partial(middle_kernel, zs), out_shape=jax.ShapeD...  132 us
    pallas_call x1, Pallas kernels, front_gather(): pl.pallas_call(functools.partial(front_kernel, zs, col_block), out_shape=...  121 us
    pallas_call x1, Pallas kernels, ladder_tail(): pl.pallas_call(tail_kernel, out_shape=(jax.ShapeDtypeStruct((rows, pairs,...  95.3 us
    unnamed x3, local copies, waits for them, and re-layouts  9.97 us

profile of v5, /device:TPU:0, one launch (start us, length us, event | category | flops | bytes accessed | tf_op | source)
XLA Modules:
  0.0 368.6 jit_solution(2342081028643300040)
XLA Ops:
  0.6 0.0 copy-start
  0.6 0.8 dynamic_slice.3
  1.4 1.3 broadcast_in_dim.2.virt_ref
  2.7 2.0 pad.8.own_ref
  4.7 1.3 pad.9
  6.0 1.6 reshape.60.amp_ref
  7.5 0.0 copy-done
  7.5 1.2 broadcast_subtract_fusion.rowen_ref
  8.7 121.1 %shard_map.77 = (bf16[4,304,1024]{2,1,0:T(8,128)(2,1)}, bf16[8,4,304,256]{3,2,1,0:T(8,128)(2,1)}, bf16[4,1024,256]{2,1,0:T(8,128)(2,1)}, bf16[4,2,304,1024]{3,2,1,0:T(8,128)(2,1)}, bf16[1024,1200]{1,0:T(8,128)(2,1)}) custom-call(bf16[304,1024]{1,0:T(8,128)(2,1)} %pad.8.own_ref, bf16[160,2560]{1,0:T(8,128)(2,1)} %reshape.60.amp_ref, bf16[2048,1024]{1,0:T(8,128)(2,1)} %kern_ref.3), custom_call_target="tpu_custom_call" | custom-call | flops 10000000000 | bytes 10000000 | tf_op jit(solution)/shard_map/pallas_call | solution.py:509
  129.8 131.8 %shard_map.78.back_ref = bf16[8,4,304,256]{3,2,1,0:T(8,128)(2,1)} custom-call(bf16[4,304,1024]{2,1,0:T(8,128)(2,1)} %get-tuple-element.9.cols_ref, bf16[4,2,304,1024]{3,2,1,0:T(8,128)(2,1)} %get-tuple-element.10.line_ref, bf16[8,4,304,256]{3,2,1,0:T(8,128)(2,1)} %get-tuple-element.11.half_ref, bf16[2048,1024]{1,0:T(8,128)(2,1)} %kern_ref.3, ...), custom_call_target="tpu_custom_call" | custom-call | flops 81604378624 | bytes 39845888 | tf_op jit(solution)/shard_map/pallas_call | solution.py:559
  261.6 95.3 %shard_map.79 = (f32[300,8,1200]{2,1,0:T(8,128)}, f32[1,1]{1,0:T(1,128)}) custom-call(bf16[8,4,304,256]{3,2,1,0:T(8,128)(2,1)} %shard_map.78.back_ref, bf16[1024,1200]{1,0:T(8,128)(2,1)} %get-tuple-element.13.turned, f32[300,8,1200]{2,1,0:T(8,128)} %bitcast.6, f32[8,300,1]{2,1,0:T(8,128)} %broadcast_subtract_fusion.rowen_ref, f32[1,1200]{1,0:T(1,128)} %broadcast_in_dim.2.virt_ref), custom_call_target="tpu_custom_call" | custom-call | flops 5898240000 | bytes 23040000 | tf_op jit(solution)/shard_map/pallas_call | solution.py:781
  357.5 10.0 %copy.9 = f32[8,300,1200]{2,0,1:T(8,128)} copy(f32[8,300,1200]{2,0,1:T(8,128)} %bitcast.4) | data formatting | bytes 23040000
Async XLA Ops:
  0.6 6.9 %copy-start = (f32[8]{0:T(128)S(1)}, f32[8]{0:T(128)}, u32[]{:S(2)}) copy-start(f32[8]{0:T(128)} %param.11) | copy-start | bytes 100
